TPU v7x, 32 devices: a whole 2x2x4 slice. The times are simulated.
32 devices in a mesh: gz: 8 (over z, y), gy: 4 (over x, core).
Axes of the slice: x: 2, y: 2, z: 4, core: 2. Of those that a mesh axis runs over, the one named last changes fastest.
Arguments:
- orbitals: bfloat16 [96, 96, 96, 256], P('gz', 'gy'), may hold values from -6 to 6
- pair_list: int32 [64, 2], replicated, may hold values from 0 to 255
- box_anchor: int32 [256, 3], replicated, may hold values from 0 to 95
- pair_live: int32 [64], replicated, may hold values from 0 to 1, as said below
Outputs:
- gradient: float32 [96, 96, 96, 256], P('gz', 'gy')
Inputs may be any that keep to these rules, and one draw needn't show every extreme that they name: `pair_live`: in each owner's block of 2 slots the live slots come first; at least one slot of every block is live, some block has all 2 live, and some other block has exactly one live.
All inputs are finite; a program needn't handle non-finite values.
Results may differ from a plain program's by a relative error of at most 0.0035.
Values may be sent and summed in bfloat16 or wider, within the bound.
A program may use at most 192 MiB of HBM per device.

v0:
```python
import jax
import jax.numpy as jnp
from jax import lax
from jax.sharding import PartitionSpec as P

B = 64


def poisson_box(density):
    side = density.shape[-1]
    index = jnp.arange(1, side + 1).astype(jnp.float32)
    table = jnp.sqrt(2.0 / (side + 1.0)) * jnp.sin(
        jnp.pi * index[:, None] * index[None, :] / (side + 1.0)
    )
    eigen = 2.0 - 2.0 * jnp.cos(jnp.pi * index / (side + 1.0))
    denom = eigen[:, None, None] + eigen[None, :, None] + eigen[None, None, :]
    hp = lax.Precision.HIGHEST

    def apply_all(field):
        field = jnp.einsum("...abc,ai->...ibc", field, table, precision=hp)
        field = jnp.einsum("...ibc,bj->...ijc", field, table, precision=hp)
        return jnp.einsum("...ijc,ck->...ijk", field, table, precision=hp)

    return apply_all(apply_all(density) / denom)


def body(orbitals, pair_list, box_anchor, pair_live):
    depth, rows, across, norb = orbitals.shape
    n_gz = lax.axis_size("gz")
    n_gy = lax.axis_size("gy")
    owners = n_gz * n_gy
    pairs = pair_list.shape[0]
    per_dev = pairs // owners
    slots = 2 * per_dev
    side = B
    extent = depth * n_gz
    firsts = pair_list[:, 0]
    chosen = jnp.take(orbitals, pair_list.reshape(-1), axis=3)
    width = chosen.shape[2]
    outgoing = chosen.reshape(depth, rows, width, n_gz, n_gy, slots)
    flat_send = outgoing.reshape(depth, rows, width, owners, slots)
    incoming = lax.all_to_all(
        flat_send, ("gz", "gy"), split_axis=3, concat_axis=3, tiled=True
    ).reshape(depth, rows, width, n_gz, n_gy, slots)
    grids = jnp.transpose(incoming, (5, 3, 0, 4, 1, 2)).reshape(per_dev, 2, extent, extent, width)
    owner = lax.axis_index(("gz", "gy"))
    mine = lax.dynamic_slice_in_dim(pair_list, owner * per_dev, per_dev, 0)
    live = lax.dynamic_slice_in_dim(pair_live, owner * per_dev, per_dev, 0)
    anchors = box_anchor[mine[:, 0]]

    def cut_box(grid, anchor):
        grid = jnp.roll(grid, -anchor[0], axis=0)
        grid = jnp.roll(grid, -anchor[1], axis=1)
        grid = jnp.roll(grid, -anchor[2], axis=2)
        return grid[:side, :side, :side]

    def both_boxes(pair_grids, anchor):
        return jax.vmap(cut_box, in_axes=(0, None))(pair_grids, anchor)

    boxes = jax.vmap(both_boxes)(grids, anchors)
    left = boxes[:, 0].astype(jnp.float32)
    right = boxes[:, 1].astype(jnp.float32)
    potential = poisson_box(left * right)
    weight = live.astype(jnp.float32)[:, None, None, None]
    term = (potential * right * weight).astype(jnp.bfloat16)

    def place_box(box, anchor):
        pad_x = across - side
        grid = jnp.pad(box, ((0, extent - side), (0, extent - side), (0, pad_x)))
        grid = jnp.roll(grid, anchor[0], axis=0)
        grid = jnp.roll(grid, anchor[1], axis=1)
        grid = jnp.roll(grid, anchor[2], axis=2)
        return grid

    placed = jax.vmap(place_box)(term, anchors)
    back_send = jnp.transpose(
        placed.reshape(per_dev, n_gz, depth, n_gy, rows, width), (2, 4, 5, 1, 3, 0)
    )
    flat_back = back_send.reshape(depth, rows, width, owners, per_dev)
    back = lax.all_to_all(flat_back, ("gz", "gy"), split_axis=3, concat_axis=3, tiled=True)
    contrib = back.reshape(depth, rows, width, pairs)
    selector = (firsts[:, None] == jnp.arange(norb)[None, :]).astype(jnp.bfloat16)
    action = jnp.dot(contrib.reshape(-1, pairs), selector, preferred_element_type=jnp.float32)
    action_low = action.astype(jnp.bfloat16)
    flat = orbitals.reshape(-1, norb)
    partial_tiles = lax.dot_general(
        flat, action_low, (((0,), (0,)), ((), ())), preferred_element_type=jnp.float32
    )
    summed = lax.psum(partial_tiles, ("gz", "gy"))
    tiles = (summed / (float(B) ** 3 / 4.0)).astype(jnp.bfloat16)
    gradient = action - jnp.dot(flat, tiles, preferred_element_type=jnp.float32)
    return gradient.reshape(depth, rows, across, norb)


def solution(mesh):
    return jax.shard_map(
        body,
        mesh=mesh,
        in_specs=(P("gz", "gy", None, None), P(), P(), P()),
        out_specs=P("gz", "gy", None, None),
        check_vma=False,
    )
```

profile of v0, /device:TPU:0, one launch (start us, length us, event | category | flops | bytes accessed | tf_op | source)
XLA Modules:
  0.0 841.9 jit_solution(8082996493727971002)
XLA Ops:
  7.5 22.4 %copy.44 = bf16[12,24,96,256]{2,1,0,3:T(8,128)(2,1)} copy(bf16[12,24,96,256]{3,2,1,0:T(8,128)(2,1)} %param.4) | data formatting | bytes 28311552 | tf_op args[0]
  29.9 13.6 %gather_fusion = bf16[128,12,24,96]{3,2,1,0:T(8,128)(2,1)} fusion(bf16[12,24,96,256]{2,1,0,3:T(8,128)(2,1)} %copy.44, s32[1024]{0:T(1024)S(1)} %pad_clamp_fusion.1), kind=kCustom, calls=%fused_computation | custom fusion | bytes 14156288 | tf_op jit(solution)/shard_map/jit(_take)/gather | solution.py:38
  43.5 9.6 %copy.45 = bf16[12,24,96,128]{2,1,3,0:T(8,128)(2,1)} copy(bf16[12,24,96,128]{2,1,0,3:T(8,128)(2,1)} %bitcast.113) | data formatting | bytes 14155776 | tf_op jit(solution)/shard_map/jit(_take)/gather | solution.py:38
  53.2 8.6 %broadcast_select_fusion = bf16[12,24,96,32,4]{2,1,4,3,0:T(8,128)(2,1)} fusion(bf16[12,24,96,32,4]{2,1,4,3,0:T(8,128)(2,1)} %bitcast.112, pred[32,4]{1,0:T(8,128)(4,1)S(1)} %compare_and_fusion), kind=kLoop, calls=%fused_computation.24 | loop fusion | flops 3538944 | bytes 14155904 | tf_op jit(solution)/shard_map/jit(_take)/select_n | solution.py:38
  61.7 10.2 %copy.46 = bf16[12,24,96,32,4]{2,1,4,0,3:T(8,128)(2,1)} copy(bf16[12,24,96,32,4]{2,1,4,3,0:T(8,128)(2,1)} %broadcast_select_fusion) | data formatting | bytes 14155776 | tf_op jit(solution)/shard_map/jit(_take)/select_n | solution.py:38
  71.9 7.6 all-to-all-start
  81.5 206.9 %all-to-all-done = bf16[12,24,96,32,4]{2,1,4,0,3:T(8,128)(2,1)} async-done(((bf16[12,24,96,32,4]{2,1,4,0,3:T(8,128)(2,1)}), bf16[12,24,96,32,4]{2,1,4,0,3:T(8,128)(2,1)}, u32[]{:S(2)}, u32[]{:S(2)}) %all-to-all-start) | async-done | bytes 7077920 | tf_op jit(solution)/shard_map/all_to_all | solution.py:42
  288.4 10.2 %copy.48 = bf16[4,8,12,4,24,96]{5,4,3,2,1,0:T(8,128)(2,1)} copy(bf16[4,8,12,4,24,96]{5,4,0,2,3,1:T(8,128)(2,1)} %bitcast.9) | data formatting | bytes 14155776 | tf_op jit(solution)/shard_map/transpose | solution.py:45
  298.6 16.0 %pad_maximum_fusion = bf16[2,2,192,96,96]{4,3,2,1,0:T(8,128)(2,1)} fusion(bf16[2,2,96,96,96]{4,3,2,1,0:T(8,128)(2,1)} %bitcast.111), kind=kLoop, calls=%fused_computation.16 | loop fusion | flops 7077888 | bytes 21233664 | tf_op jit(solution)/shard_map/vmap(vmap(jit(_roll_dynamic)))/concatenate | solution.py:52
  319.8 14.5 %while.6 = (s32[]{:T(128)}, bf16[2,2,192,96,96]{4,3,2,1,0:T(8,128)(2,1)}, s32[2,4]{1,0:T(2,128)S(1)}, bf16[2,2,96,96,96]{4,3,2,1,0:T(8,128)(2,1)}, s32[]{:T(128)}) while((s32[]{:T(128)}, bf16[2,2,192,96,96]{4,3,2,1,0:T(8,128)(2,1)}, s32[2,4]{1,0:T(2,128)S(1)}, bf16[2,2,96,96,96]{4,3,2,1,0:T(8,128)(2,1)}, s32[]{:T(128)}) %tuple.99), condition=%wide.while_cond, body=%wide.while_body.sunk | while | flops 2 | bytes 9438833 | solution.py:52
  320.4 6.7 dynamic-slice_dynamic-update-slice_fusion.10
  334.3 18.2 %pad_maximum_fusion.1 = bf16[2,2,96,192,96]{4,3,2,1,0:T(8,128)(2,1)} fusion(bf16[2,2,96,96,96]{4,3,2,1,0:T(8,128)(2,1)} %get-tuple-element.12), kind=kLoop, calls=%fused_computation.17 | loop fusion | flops 28311552 | bytes 21233664 | tf_op jit(solution)/shard_map/vmap(vmap(jit(_roll_dynamic)))/concatenate | solution.py:53
  357.6 18.6 %while.7 = (s32[]{:T(128)}, bf16[2,2,96,192,96]{4,3,2,1,0:T(8,128)(2,1)}, s32[2,4]{1,0:T(2,128)S(1)}, bf16[2,2,96,96,96]{4,3,2,1,0:T(8,128)(2,1)}, s32[]{:T(128)}) while((s32[]{:T(128)}, bf16[2,2,96,192,96]{4,3,2,1,0:T(8,128)(2,1)}, s32[2,4]{1,0:T(2,128)S(1)}, bf16[2,2,96,96,96]{4,3,2,1,0:T(8,128)(2,1)}, s32[]{:T(128)}) %tuple.102), condition=%wide.while_cond.1, body=%wide.while_body.1.sunk | while | flops 2 | bytes 9438833 | solution.py:53
  358.3 8.7 %dynamic-slice_dynamic-update-slice_fusion.11 = bf16[2,2,96,96,96]{4,3,2,1,0:T(8,128)(2,1)} fusion(bf16[2,2,96,96,96]{4,3,2,1,0:T(8,128)(2,1)} %get-tuple-element.323, s32[]{:T(128)} %get-tuple-element.320, bf16[2,2,96,192,96]{4,3,2,1,0:T(8,128)(2,1)} %get-tuple-element.326, s32[]{:T(128)} %bitcast.98, s32[]{:T(128)} %bitcast.99), kind=kLoop, calls=%fused_computation.4.clone.1 | loop fusion | bytes 9438720 | tf_op jit(solution)/shard_map/vmap(vmap(jit(_roll_dynamic)))/gather
  367.7 8.6 %dynamic-slice_dynamic-update-slice_fusion.11 = bf16[2,2,96,96,96]{4,3,2,1,0:T(8,128)(2,1)} fusion(bf16[2,2,96,96,96]{4,3,2,1,0:T(8,128)(2,1)} %get-tuple-element.323, s32[]{:T(128)} %get-tuple-element.320, bf16[2,2,96,192,96]{4,3,2,1,0:T(8,128)(2,1)} %get-tuple-element.326, s32[]{:T(128)} %bitcast.98, s32[]{:T(128)} %bitcast.99), kind=kLoop, calls=%fused_computation.4.clone.1 | loop fusion | bytes 9438720 | tf_op jit(solution)/shard_map/vmap(vmap(jit(_roll_dynamic)))/gather
  376.3 20.0 %pad_maximum_fusion.2 = bf16[2,2,96,96,192]{4,3,2,1,0:T(8,128)(2,1)} fusion(bf16[2,2,96,96,96]{4,3,2,1,0:T(8,128)(2,1)} %get-tuple-element.20), kind=kLoop, calls=%fused_computation.18 | loop fusion | flops 28311552 | bytes 21233664 | tf_op jit(solution)/shard_map/vmap(vmap(jit(_roll_dynamic)))/concatenate | solution.py:54
  396.3 19.1 %while.8 = (s32[]{:T(128)}, bf16[2,2,96,96,192]{4,3,2,1,0:T(8,128)(2,1)}, s32[2,4]{1,0:T(2,128)S(1)}, bf16[2,2,96,96,96]{4,3,2,0,1:T(8,128)(2,1)}, s32[]{:T(128)}) while((s32[]{:T(128)}, bf16[2,2,96,96,192]{4,3,2,1,0:T(8,128)(2,1)}, s32[2,4]{1,0:T(2,128)S(1)}, bf16[2,2,96,96,96]{4,3,2,0,1:T(8,128)(2,1)}, s32[]{:T(128)}) %tuple.105), condition=%wide.while_cond.2, body=%wide.while_body.2.sunk | while | flops 2 | bytes 9438833 | solution.py:54
  396.9 8.7 %bitcast_dynamic-update-slice_fusion.2 = bf16[2,2,96,96,96]{4,3,2,0,1:T(8,128)(2,1)} fusion(bf16[2,2,96,96,96]{4,3,2,0,1:T(8,128)(2,1)} %get-tuple-element.338, s32[]{:T(128)} %get-tuple-element.335, bf16[2,2,96,96,192]{4,3,2,1,0:T(8,128)(2,1)} %get-tuple-element.341, s32[]{:T(128)} %bitcast.101, s32[]{:T(128)} %bitcast.102), kind=kLoop, calls=%fused_computation.6.clone.1 | loop fusion | bytes 9438720 | tf_op jit(solution)/shard_map/vmap(vmap(jit(_roll_dynamic)))/gather
  406.2 8.8 %bitcast_dynamic-update-slice_fusion.2 = bf16[2,2,96,96,96]{4,3,2,0,1:T(8,128)(2,1)} fusion(bf16[2,2,96,96,96]{4,3,2,0,1:T(8,128)(2,1)} %get-tuple-element.338, s32[]{:T(128)} %get-tuple-element.335, bf16[2,2,96,96,192]{4,3,2,1,0:T(8,128)(2,1)} %get-tuple-element.341, s32[]{:T(128)} %bitcast.101, s32[]{:T(128)} %bitcast.102), kind=kLoop, calls=%fused_computation.6.clone.1 | loop fusion | bytes 9438720 | tf_op jit(solution)/shard_map/vmap(vmap(jit(_roll_dynamic)))/gather
  425.0 6.6 fusion.13
  441.8 6.6 fusion.9
  461.8 10.2 %while.9 = (s32[]{:T(128)}, bf16[2,192,96,96]{3,2,1,0:T(8,128)(2,1)}, s32[2,4]{1,0:T(2,128)S(1)}, bf16[2,96,96,96]{3,2,1,0:T(8,128)(2,1)}, s32[]{:T(128)}) while((s32[]{:T(128)}, bf16[2,192,96,96]{3,2,1,0:T(8,128)(2,1)}, s32[2,4]{1,0:T(2,128)S(1)}, bf16[2,96,96,96]{3,2,1,0:T(8,128)(2,1)}, s32[]{:T(128)}) %tuple.108), condition=%wide.while_cond.3, body=%wide.while_body.3.sunk | while | flops 2 | bytes 4720241 | solution.py:70
  472.0 10.1 %pad_maximum_fusion.4 = bf16[2,96,192,96]{3,2,1,0:T(8,128)(2,1)} fusion(bf16[2,96,96,96]{3,2,1,0:T(8,128)(2,1)} %get-tuple-element.36), kind=kLoop, calls=%fused_computation.22 | loop fusion | flops 14155776 | bytes 10616832 | tf_op jit(solution)/shard_map/vmap(jit(_roll_dynamic))/concatenate | solution.py:71
  484.8 12.6 %while.10 = (s32[]{:T(128)}, bf16[2,96,192,96]{3,2,1,0:T(8,128)(2,1)}, s32[2,4]{1,0:T(2,128)S(1)}, bf16[2,96,96,96]{3,2,1,0:T(8,128)(2,1)}, s32[]{:T(128)}) while((s32[]{:T(128)}, bf16[2,96,192,96]{3,2,1,0:T(8,128)(2,1)}, s32[2,4]{1,0:T(2,128)S(1)}, bf16[2,96,96,96]{3,2,1,0:T(8,128)(2,1)}, s32[]{:T(128)}) %tuple.111), condition=%wide.while_cond.4, body=%wide.while_body.4.sunk | while | flops 2 | bytes 4720241 | solution.py:71
  497.4 11.6 %pad_maximum_fusion.5 = bf16[2,96,96,192]{3,2,1,0:T(8,128)(2,1)} fusion(bf16[2,96,96,96]{3,2,1,0:T(8,128)(2,1)} %get-tuple-element.44), kind=kLoop, calls=%fused_computation.23 | loop fusion | flops 14155776 | bytes 10616832 | tf_op jit(solution)/shard_map/vmap(jit(_roll_dynamic))/concatenate | solution.py:72
  511.7 12.9 %while.11 = (s32[]{:T(128)}, bf16[2,96,96,192]{3,2,1,0:T(8,128)(2,1)}, s32[2,4]{1,0:T(2,128)S(1)}, bf16[2,96,96,96]{3,2,1,0:T(8,128)(2,1)}, s32[]{:T(128)}) while((s32[]{:T(128)}, bf16[2,96,96,192]{3,2,1,0:T(8,128)(2,1)}, s32[2,4]{1,0:T(2,128)S(1)}, bf16[2,96,96,96]{3,2,1,0:T(8,128)(2,1)}, s32[]{:T(128)}) %tuple.114), condition=%wide.while_cond.5, body=%wide.while_body.5.sunk | while | flops 2 | bytes 4720241 | solution.py:72
  535.5 105.1 %all-to-all-done.1 = bf16[12,24,96,32,2]{2,1,4,0,3:T(8,128)(2,1)} async-done(((bf16[12,24,96,32,2]{2,1,4,0,3:T(8,128)(2,1)}), bf16[12,24,96,32,2]{2,1,4,0,3:T(8,128)(2,1)}, u32[]{:S(2)}, u32[]{:S(2)}) %all-to-all-start.1) | async-done | bytes 3538976 | tf_op jit(solution)/shard_map/all_to_all | solution.py:80
  645.9 8.1 reshape_reshape.4
  654.0 12.0 %fusion.32 = f32[27648,256]{1,0:T(8,128)} fusion(bf16[27648,64]{0,1:T(8,128)(2,1)S(1)} %reshape_reshape.4, s32[64]{0:T(128)S(1)} %slice_bitcast_fusion), kind=kOutput, calls=%fused_computation.49 | convolution fusion | flops 905986048 | bytes 31850752 | tf_op jit(solution)/shard_map/dot_general | solution.py:83
  666.0 17.6 %fusion.28 = f32[256,256]{0,1:T(8,128)} fusion(bf16[27648,256]{1,0:T(8,128)(2,1)} %bitcast.109, f32[27648,256]{1,0:T(8,128)} %fusion.32), kind=kOutput, calls=%fused_computation.44 | convolution fusion | flops 3630956544 | bytes 42729472 | tf_op jit(solution)/shard_map/dot_general | solution.py:86
  683.7 126.0 %all-reduce.7.cloned.1.call-done = f32[256,256]{0,1:T(8,128)} async-done(((f32[256,256]{0,1:T(8,128)}), f32[256,256]{0,1:T(8,128)}) %all-reduce.7.cloned.1.call-update) | async-done | bytes 262160 | tf_op jit(solution)/shard_map/psum | solution.py:89
  809.6 25.2 %fusion = f32[27648,256]{1,0:T(8,128)} fusion(f32[27648,256]{1,0:T(8,128)} %fusion.32, bf16[27648,256]{1,0:T(8,128)(2,1)} %bitcast.110, f32[256,256]{0,1:T(8,128)} %all-reduce.7.cloned.1.call-done), kind=kOutput, calls=%fused_computation.15 | convolution fusion | flops 3631087616 | bytes 71041024 | tf_op jit(solution)/shard_map/dot_general | solution.py:91
  (79 shorter events, 113.6 us)
Async XLA Ops:
  71.9 7.7 copy-start
  71.9 8.6 %copy-start.2 = (s32[64]{0:T(128)S(1)}, s32[64]{0:T(128)}, u32[]{:S(2)}) copy-start(s32[64]{0:T(128)} %param.7) | copy-start | bytes 772
  71.9 216.5 %all-to-all-start = ((bf16[12,24,96,32,4]{2,1,4,0,3:T(8,128)(2,1)}), bf16[12,24,96,32,4]{2,1,4,0,3:T(8,128)(2,1)}, u32[]{:S(2)}, u32[]{:S(2)}) async-start(bf16[12,24,96,32,4]{2,1,4,0,3:T(8,128)(2,1)} %copy.46), calls=%async_computation | async-start | bytes 18874368 | tf_op jit(solution)/shard_map/all_to_all | solution.py:42
  528.2 7.2 copy-start.1
  531.8 108.8 %all-to-all-start.1 = ((bf16[12,24,96,32,2]{2,1,4,0,3:T(8,128)(2,1)}), bf16[12,24,96,32,2]{2,1,4,0,3:T(8,128)(2,1)}, u32[]{:S(2)}, u32[]{:S(2)}) async-start(bf16[12,24,96,32,2]{2,1,4,0,3:T(8,128)(2,1)} %copy.62), calls=%async_computation.1 | async-start | bytes 9437184 | tf_op jit(solution)/shard_map/all_to_all | solution.py:80
  535.4 274.2 %all-reduce.7.cloned.1.call-start = ((), (), s32[]{:S(2)}) async-start(), calls=%async_computation.2 | async-start | bytes 524288 | tf_op jit(solution)/shard_map/psum | solution.py:89
Sparse Core Ops, SparseCore 0:
  683.8 125.7 all-reduce.6
where the time goes:
time: 849 us; the launch traced here: 842 us
  waiting for transfers between devices  438 us (52%)
  local copies, waits for them, and re-layouts  195 us (23%)
  other arithmetic  93.4 us (11%)
  matrix products  90 us (11%)
  between operations  13.8 us (2%)
  starting transfers between devices  11.2 us (1%)
    all_to_all x1, waiting for transfers between devices, body(): lax.all_to_all(flat_send, ('gz', 'gy'), split_axis=3, concat_axis=3, tile...  207 us
    psum x1, waiting for transfers between devices, body(): summed = lax.psum(partial_tiles, ('gz', 'gy'))  126 us
    all_to_all x1, waiting for transfers between devices, body(): lax.all_to_all(flat_back, ('gz', 'gy'), split_axis=3, concat_axis=3, tile...  105 us
    gather x36, local copies, waits for them, and re-layouts  87.1 us
    unnamed x15, local copies, waits for them, and re-layouts  41.7 us
    dot_general x1, matrix products, body(): gradient = action - jnp.dot(flat, tiles, preferred_element_type=jnp.float32)  25.2 us
    gather x2, local copies, waits for them, and re-layouts, body(): chosen = jnp.take(orbitals, pair_list.reshape(-1), axis=3)  23.2 us
    concatenate x1, other arithmetic, cut_box(): grid = jnp.roll(grid, -anchor[2], axis=2)  20 us
  transfers between devices with their start and end apart: 3, of which 3 were waited for; matrix products, arithmetic and copies ran while one was open for 0% of the time, Pallas kernels for 0%

commit v1 on v0

v1 whole, which is shorter than its diff:
```python
import functools

import jax
import jax.numpy as jnp
import numpy as np
from jax import lax
from jax.experimental import pallas as pl
from jax.experimental.pallas import tpu as pltpu
from jax.sharding import PartitionSpec as P

B = 64
LANES = 128
BF = jnp.bfloat16
F32 = jnp.float32
VMEM_LIMIT = 56 * 1024 * 1024


def dot_nt(a, b):
    return lax.dot_general(a, b, (((1,), (1,)), ((), ())), preferred_element_type=F32)


def dot_nn(a, b):
    return lax.dot_general(a, b, (((1,), (0,)), ((), ())), preferred_element_type=F32)


def dot_tn(a, b):
    return lax.dot_general(a, b, (((0,), (0,)), ((), ())), preferred_element_type=F32)


def split(a):
    hi = a.astype(BF)
    return hi, (a - hi.astype(F32)).astype(BF)


def density_kernel(per_dev, ax_ref, onehot_ref, orb_ref, out_ref, scr):
    _, rows, across, _ = orb_ref.shape
    pairs = onehot_ref.shape[0] // 2
    owners = pairs // per_dev

    def row(y, _):
        both = dot_nt(onehot_ref[...], orb_ref[0, y])
        scr[pl.ds(pl.multiple_of(y * pairs, 8), pairs), :across] = both[:pairs] * both[pairs:]
        return 0

    lax.fori_loop(0, rows, row, 0, unroll=4)
    lane = lax.broadcasted_iota(jnp.int32, (rows, LANES), 1)

    def owner(d, _):
        acc = jnp.zeros((rows, LANES), F32)
        for s in range(per_dev):
            p = d * per_dev + s
            a = ax_ref[p]
            base = s * B
            x = scr[pl.ds(p, rows, stride=pairs), :]
            near = pltpu.roll(x, lax.rem(base - a + 2 * LANES, LANES), 1)
            far = pltpu.roll(x, lax.rem(base + across - a + 2 * LANES, LANES), 1)
            rel = lane - base
            acc = jnp.where((rel >= 0) & (rel < B), jnp.where(rel < across - a, near, far), acc)
        out_ref[d, 0] = acc.astype(BF)
        return 0

    lax.fori_loop(0, owners, owner, 0, unroll=4)


def poisson_kernel(per_dev, extent, az_ref, ay_ref, ly_ref, left_ref, sx2_ref, sx3_ref, lzx_ref, in_ref, out_ref, field, ring):
    n_gz, n_gy, depth, rows, _ = in_ref.shape
    lane = lax.broadcasted_iota(jnp.int32, (B, LANES), 1)
    lane_all = lax.broadcasted_iota(jnp.int32, (extent, LANES), 1)
    slots = ring.shape[0]

    def along_rows(e):
        hi, lo = split(e)
        return dot_nn(left_ref[...], jnp.concatenate([hi, hi, lo], axis=0))

    def cut(a, slot):
        out = None
        for s in range(per_dev):
            z = lax.rem(az_ref[s] + a, extent)
            gz = z // depth
            zi = z - gz * depth
            for gy in range(n_gy):
                part = in_ref[gz, gy, zi].astype(F32)
                ring[slot, s, gy * rows:(gy + 1) * rows] = part
                ring[slot, s, extent + gy * rows:extent + (gy + 1) * rows] = part
            got = ring[slot, s, pl.ds(ay_ref[s], B), :]
            out = got if out is None else jnp.where(lane >= s * B, got, out)
        return out

    def first(step, _):
        for slot in range(slots):
            a = step * slots + slot
            d = cut(a, slot).astype(BF)
            e = dot_nn(jnp.concatenate([d, d], axis=1), sx2_ref[...])
            field[pl.ds(pl.multiple_of(a * B, 8), B), :] = along_rows(e)
        return 0

    lax.fori_loop(0, B // slots, first, 0)

    def middle(step, _):
        for k in range(4):
            y = step * 4 + k
            e = along_rows(field[pl.ds(y, B, stride=B), :])
            e = e / (lzx_ref[...] + ly_ref[y])
            field[pl.ds(y, B, stride=B), :] = along_rows(e)
        return 0

    lax.fori_loop(0, B // 4, middle, 0)

    def last(step, _):
        for k in range(4):
            a = step * 4 + k
            at = pl.ds(pl.multiple_of(a * B, 8), B)
            hi, lo = split(along_rows(field[at, :]))
            field[at, :] = dot_nn(jnp.concatenate([hi, hi, lo], axis=1), sx3_ref[...])
        return 0

    lax.fori_loop(0, B // 4, last, 0)
    ring[...] = jnp.zeros_like(ring)

    def place(step, _):
        for slot in range(slots):
            z = step * slots + slot
            out = jnp.zeros((extent, LANES), F32)
            for s in range(per_dev):
                a = lax.rem(z - az_ref[s] + extent, extent)
                v = field[pl.ds(pl.multiple_of(jnp.minimum(a, B - 1) * B, 8), B), :]
                v = jnp.where(a < B, v, 0.0)
                ring[slot, s, :B] = v
                ring[slot, s, extent:extent + B] = v
                got = ring[slot, s, pl.ds(extent - ay_ref[s], extent), :]
                out = jnp.where(lane_all >= s * B, got, out)
            gz = z // depth
            zi = z - gz * depth
            for gy in range(n_gy):
                out_ref[gz, gy, zi] = out[gy * rows:(gy + 1) * rows].astype(BF)
        return 0

    lax.fori_loop(0, extent // slots, place, 0)


def term_kernel(per_dev, ax_ref, live_ref, onehot_ref, same_ref, orb_ref, in_ref, term_ref, tile_ref, scr):
    _, rows, across, _ = orb_ref.shape
    pairs = onehot_ref.shape[0]
    owners = pairs // per_dev
    lane = lax.broadcasted_iota(jnp.int32, (rows, LANES), 1)

    def owner(d, _):
        v = in_ref[d, 0].astype(F32)
        for s in range(per_dev):
            p = d * per_dev + s
            a = ax_ref[p]
            base = s * B
            near = pltpu.roll(v, lax.rem(a - base + 2 * LANES, LANES), 1)
            far = pltpu.roll(v, lax.rem(a - across - base + 3 * LANES, LANES), 1)
            rel = lane - a
            lit = live_ref[p] > 0
            v_p = jnp.where((rel >= 0) & (rel < B) & lit, near, 0.0)
            v_p = jnp.where((rel + across < B) & lit, far, v_p)
            scr[pl.ds(p, rows, stride=pairs), :] = v_p
        return 0

    lax.fori_loop(0, owners, owner, 0, unroll=4)

    @pl.when(pl.program_id(0) == 0)
    def _():
        tile_ref[...] = jnp.zeros_like(tile_ref)

    step = 4 if rows % 4 == 0 else 1

    def row(i, acc):
        for k in range(step):
            y = i * step + k
            o = orb_ref[0, y]
            psi = dot_nt(onehot_ref[...], o)
            t = (scr[pl.ds(pl.multiple_of(y * pairs, 8), pairs), :across] * psi).astype(BF)
            term_ref[0, y] = t
            low = dot_nn(same_ref[...], t).astype(BF)
            acc = acc + dot_nn(low, o)
        return acc

    tile_ref[...] += lax.fori_loop(0, rows // step, row, jnp.zeros(tile_ref.shape, F32))


def gradient_kernel(sel_ref, tiles_ref, orb_ref, term_ref, out_ref):
    _, rows, _, _ = orb_ref.shape

    def row(y, _):
        out_ref[0, y] = dot_tn(term_ref[0, y], sel_ref[...]) - dot_nn(orb_ref[0, y], tiles_ref[...])
        return 0

    lax.fori_loop(0, rows, row, 0, unroll=4)


def tables(per_dev):
    index = np.arange(1, B + 1, dtype=np.float64)
    s = np.sqrt(2.0 / (B + 1.0)) * np.sin(np.pi * index[:, None] * index[None, :] / (B + 1.0))
    eigen = 2.0 - 2.0 * np.cos(np.pi * index / (B + 1.0))
    hi = s.astype(jnp.bfloat16)
    lo = (s - hi.astype(np.float64)).astype(jnp.bfloat16)
    eye = np.eye(per_dev)
    bd = lambda m: np.kron(eye, m.astype(np.float32)).astype(jnp.bfloat16)
    left = np.concatenate([hi, lo, hi], axis=1)
    sx2 = np.concatenate([bd(hi), bd(lo)], axis=0)
    sx3 = np.concatenate([bd(hi), bd(lo), bd(hi)], axis=0)
    lzx = (eigen[:, None] + np.tile(eigen, per_dev)[None, :]).astype(np.float32)
    return eigen.astype(np.float32), left, sx2, sx3, lzx


def body(orbitals, pair_list, box_anchor, pair_live):
    depth, rows, across, norb = orbitals.shape
    n_gz = lax.axis_size("gz")
    n_gy = lax.axis_size("gy")
    owners = n_gz * n_gy
    pairs = pair_list.shape[0]
    per_dev = pairs // owners
    extent = depth * n_gz
    firsts = pair_list[:, 0]
    seconds = pair_list[:, 1]
    anchors = box_anchor[firsts]
    ax = anchors[:, 2]
    me = lax.axis_index(("gz", "gy"))
    mine = lax.dynamic_slice_in_dim(anchors, me * per_dev, per_dev, 0)
    orbs = jnp.arange(norb)
    sel = firsts[:, None] == orbs[None, :]
    hot_first = sel.astype(BF)
    hot_second = (seconds[:, None] == orbs[None, :]).astype(BF)
    hot_both = jnp.concatenate([hot_first, hot_second], axis=0)
    equal = firsts[:, None] == firsts[None, :]
    same = equal.astype(BF)
    slot = jnp.arange(pairs)
    leads = jnp.logical_not(jnp.any(equal & (slot[None, :] < slot[:, None]), axis=1))
    lead_sel = (sel & leads[:, None]).astype(BF)

    smem = pl.BlockSpec(memory_space=pltpu.SMEM)
    full = lambda shape: pl.BlockSpec(shape, lambda z: (0,) * len(shape))
    orb_spec = pl.BlockSpec((1, rows, across, norb), lambda z: (z, 0, 0, 0))
    slab_spec = pl.BlockSpec((owners, 1, rows, LANES), lambda z: (0, z, 0, 0))
    slab = jax.ShapeDtypeStruct((owners, depth, rows, LANES), BF)
    params = pltpu.CompilerParams(dimension_semantics=("arbitrary",), vmem_limit_bytes=VMEM_LIMIT)

    density = pl.pallas_call(
        functools.partial(density_kernel, per_dev),
        grid=(depth,),
        out_shape=slab,
        in_specs=[smem, full((2 * pairs, norb)), orb_spec],
        out_specs=slab_spec,
        scratch_shapes=[pltpu.VMEM((rows * pairs, LANES), F32)],
        compiler_params=params,
        name="density",
    )(ax, hot_both, orbitals)
    incoming = lax.all_to_all(density, ("gz", "gy"), split_axis=0, concat_axis=0, tiled=True)
    incoming = incoming.reshape(n_gz, n_gy, depth, rows, LANES)

    eigen, left, sx2, sx3, lzx = tables(per_dev)
    vmem = pl.BlockSpec(memory_space=pltpu.VMEM)
    potential = pl.pallas_call(
        functools.partial(poisson_kernel, per_dev, extent),
        out_shape=jax.ShapeDtypeStruct(incoming.shape, BF),
        in_specs=[smem, smem, smem, vmem, vmem, vmem, vmem, vmem],
        out_specs=vmem,
        scratch_shapes=[
            pltpu.VMEM((B * B, LANES), F32),
            pltpu.VMEM((4, per_dev, 2 * extent, LANES), F32),
        ],
        compiler_params=pltpu.CompilerParams(vmem_limit_bytes=VMEM_LIMIT),
        name="poisson",
    )(mine[:, 0], mine[:, 1], jnp.asarray(eigen), jnp.asarray(left), jnp.asarray(sx2), jnp.asarray(sx3), jnp.asarray(lzx), incoming)
    back = lax.all_to_all(potential.reshape(owners, depth, rows, LANES), ("gz", "gy"), split_axis=0, concat_axis=0, tiled=True)

    term, part = pl.pallas_call(
        functools.partial(term_kernel, per_dev),
        grid=(depth,),
        out_shape=(
            jax.ShapeDtypeStruct((depth, rows, pairs, across), BF),
            jax.ShapeDtypeStruct((pairs, norb), F32),
        ),
        in_specs=[smem, smem, full((pairs, norb)), full((pairs, pairs)), orb_spec, slab_spec],
        out_specs=(
            pl.BlockSpec((1, rows, pairs, across), lambda z: (z, 0, 0, 0)),
            full((pairs, norb)),
        ),
        scratch_shapes=[pltpu.VMEM((rows * pairs, LANES), F32)],
        compiler_params=params,
        name="term",
    )(ax, pair_live, hot_second, same, orbitals, back)
    summed = lax.psum(part, ("gz", "gy"))
    rows_of = (summed / (float(B) ** 3 / 4.0)).astype(BF)
    tiles = dot_tn(rows_of, lead_sel).astype(BF)

    return pl.pallas_call(
        gradient_kernel,
        grid=(depth,),
        out_shape=jax.ShapeDtypeStruct(orbitals.shape, F32),
        in_specs=[
            full((pairs, norb)),
            full((norb, norb)),
            orb_spec,
            pl.BlockSpec((1, rows, pairs, across), lambda z: (z, 0, 0, 0)),
        ],
        out_specs=orb_spec,
        compiler_params=params,
        name="gradient",
    )(hot_first, tiles, orbitals, term)


def solution(mesh):
    return jax.shard_map(
        body,
        mesh=mesh,
        in_specs=(P("gz", "gy", None, None), P(), P(), P()),
        out_specs=P("gz", "gy", None, None),
        check_vma=False,
    )
```

time: 849 us -> 436 us (0.51)
  waiting for transfers between devices: 438 us -> 226 us
  local copies, waits for them, and re-layouts: 195 us -> 5.78 us
  Pallas kernels: 0 us -> 172 us
  other arithmetic: 93.4 us -> 2.25 us
  matrix products: 90 us -> 1.74 us
    all_to_all x2, waiting for transfers between devices: 312 us -> 107 us  [the longest x1 53.6 us: body(): lax.all_to_all(density, ('gz', 'gy'), split_axis=0, concat_axis=0, tiled=...]
    pallas_call x0 -> x4, Pallas kernels: none -> 172 us  [the longest x1 81.2 us: body(): pl.pallas_call(functools.partial(term_kernel, per_dev), grid=(depth,), ou...]
    gather x39 -> x1, local copies, waits for them, and re-layouts: 111 us -> 0.6 us  [body(): anchors = box_anchor[firsts]]
    dot_general x9 -> x1, matrix products: 90 us -> 1.74 us  [dot_tn(): lax.dot_general(a, b, (((0,), (0,)), ((), ())), preferred_element_type=F32)]
    concatenate x6 -> x1, other arithmetic: 80.5 us -> 0.62 us  [body(): hot_both = jnp.concatenate([hot_first, hot_second], axis=0)]
    unnamed x15 -> x9, local copies, waits for them, and re-layouts: 41.7 us -> 3.63 us
    transpose x2 -> x0, local copies, waits for them, and re-layouts: 13.9 us -> none  [the longest x1 10.2 us: body(): jnp.transpose(incoming, (5, 3, 0, 4, 1, 2))]
    select_n x1 -> x0, local copies, waits for them, and re-layouts: 10.2 us -> none  [body(): chosen = jnp.take(orbitals, pair_list.reshape(-1), axis=3)]
where the time goes in v1:
time: 436 us; the launch traced here: 433 us
  waiting for transfers between devices  226 us (52%)
  Pallas kernels  172 us (39%)
  between operations  13.5 us (3%)
  starting transfers between devices  11.5 us (3%)
  local copies, waits for them, and re-layouts  5.78 us (1%)
    psum x1, waiting for transfers between devices, body(): summed = lax.psum(part, ('gz', 'gy'))  119 us
    pallas_call x1, Pallas kernels, body(): pl.pallas_call(functools.partial(term_kernel, per_dev), grid=(depth,), ou...  81.2 us
    all_to_all x1, waiting for transfers between devices, body(): lax.all_to_all(density, ('gz', 'gy'), split_axis=0, concat_axis=0, tiled=...  53.6 us
    all_to_all x1, waiting for transfers between devices, body(): lax.all_to_all(potential.reshape(owners, depth, rows, LANES), ('gz', 'gy'...  53.6 us
    pallas_call x1, Pallas kernels, body(): pl.pallas_call(functools.partial(density_kernel, per_dev), grid=(depth,),...  32.6 us
    pallas_call x1, Pallas kernels, body(): pl.pallas_call(functools.partial(poisson_kernel, per_dev, extent), out_sh...  31.3 us
    pallas_call x1, Pallas kernels, body(): pl.pallas_call(gradient_kernel, grid=(depth,), out_shape=jax.ShapeDtypeSt...  27.3 us
  transfers between devices with their start and end apart: 3, of which 3 were waited for; matrix products, arithmetic and copies ran while one was open for 0% of the time, Pallas kernels for 0%

profile of v1, /device:TPU:0, one launch (start us, length us, event | category | flops | bytes accessed | tf_op | source)
XLA Modules:
  0.0 433.4 jit_solution(3542809148825196626)
XLA Ops:
  6.5 0.8 slice_bitcast_fusion
  7.3 0.8 copy.11
  8.1 0.6 gather_fusion
  8.7 0.8 slice_reduce_fusion.ax_ref
  9.5 0.1 fusion.1
  9.6 0.0 copy-start.2
  9.6 0.0 copy-start.3
  9.6 0.6 pad_maximum_fusion.onehot_ref
  10.2 32.6 %density.1 = bf16[32,12,24,128]{3,2,1,0:T(8,128)(2,1)} custom-call(s32[64]{0:T(128)} %slice_reduce_fusion.ax_ref, bf16[128,256]{1,0:T(8,128)(2,1)} %pad_maximum_fusion.onehot_ref, bf16[12,24,96,256]{3,2,1,0:T(8,128)(2,1)} %orb_ref.5), custom_call_target="tpu_custom_call" | custom-call | tf_op jit(solution)/shard_map/density/pallas_call | solution.py:241
  42.9 0.0 copy-done.2
  42.9 0.0 copy-done.3
  42.9 7.3 %all-to-all-start = ((bf16[32,12,24,128]{3,2,1,0:T(8,128)(2,1)}), bf16[32,12,24,128]{3,2,1,0:T(8,128)(2,1)S(1)}, u32[]{:S(2)}, u32[]{:S(2)}) async-start(bf16[32,12,24,128]{3,2,1,0:T(8,128)(2,1)} %density.1), calls=%async_computation | async-start | bytes 4718592 | tf_op jit(solution)/shard_map/all_to_all | solution.py:251
  50.2 0.8 slice_reduce_fusion.1
  51.0 53.6 %all-to-all-done = bf16[32,12,24,128]{3,2,1,0:T(8,128)(2,1)S(1)} async-done(((bf16[32,12,24,128]{3,2,1,0:T(8,128)(2,1)}), bf16[32,12,24,128]{3,2,1,0:T(8,128)(2,1)S(1)}, u32[]{:S(2)}, u32[]{:S(2)}) %all-to-all-start) | async-done | bytes 2359328 | tf_op jit(solution)/shard_map/all_to_all | solution.py:251
  104.6 0.0 copy-start.1
  104.6 1.4 copy-done.1
  106.0 31.3 %poisson.1 = bf16[8,4,12,24,128]{4,3,2,1,0:T(8,128)(2,1)} custom-call(s32[2]{0:T(128)} %get-tuple-element.10.az_ref, s32[2]{0:T(128)} %get-tuple-element.9.ay_ref, f32[64]{0:T(128)} %constant.35.clone.ly_ref, bf16[64,192]{1,0:T(8,128)(2,1)} %constant.36.clone.left_ref, bf16[256,128]{1,0:T(8,128)(2,1)} %constant.37.clone.sx2_ref, ...), custom_call_target="tpu_custom_call" | custom-call | tf_op jit(solution)/shard_map/poisson/pallas_call | solution.py:256
  137.3 4.1 all-to-all-start.1
  141.4 0.0 all-reduce.2.cloned.1.call-start
  141.5 0.8 fusion.7
  142.3 53.6 %all-to-all-done.1.in_ref = bf16[32,12,24,128]{3,2,1,0:T(8,128)(2,1)S(1)} async-done(((bf16[32,12,24,128]{3,2,1,0:T(8,128)(2,1)}), bf16[32,12,24,128]{3,2,1,0:T(8,128)(2,1)S(1)}, u32[]{:S(2)}, u32[]{:S(2)}) %all-to-all-start.1) | async-done | bytes 2359328 | tf_op jit(solution)/shard_map/all_to_all | solution.py:268
  195.8 0.0 copy-start
  195.8 1.4 copy-done
  197.2 81.2 %term.1 = (bf16[12,24,64,96]{3,2,1,0:T(8,128)(2,1)}, f32[64,256]{1,0:T(8,128)}) custom-call(s32[64]{0:T(128)} %slice_reduce_fusion.ax_ref, s32[64]{0:T(128)} %live_ref.1, bf16[64,256]{1,0:T(8,128)(2,1)} %copy-done.3, bf16[64,64]{1,0:T(8,128)(2,1)} %get-tuple-element.15.same_ref, bf16[12,24,96,256]{3,2,1,0:T(8,128)(2,1)} %orb_ref.5, ...), custom_call_target="tpu_custom_call" | custom-call | tf_op jit(solution)/shard_map/term/pallas_call | solution.py:270
  278.4 0.0 all-reduce.2.cloned.1.call-update
  278.4 119.0 %all-reduce.2.cloned.1.call-done = f32[64,256]{1,0:T(8,128)} async-done(((f32[64,256]{1,0:T(8,128)}), f32[64,256]{1,0:T(8,128)}) %all-reduce.2.cloned.1.call-update) | async-done | bytes 65552 | tf_op jit(solution)/shard_map/psum | solution.py:286
  397.5 1.7 convolution_convert_fusion.tiles_ref
  399.2 27.3 %gradient.1 = f32[12,24,96,256]{3,2,1,0:T(8,128)} custom-call(bf16[64,256]{1,0:T(8,128)(2,1)} %copy-done.2, bf16[256,256]{1,0:T(8,128)(2,1)} %convolution_convert_fusion.tiles_ref, bf16[12,24,96,256]{3,2,1,0:T(8,128)(2,1)} %orb_ref.5, bf16[12,24,64,96]{3,2,1,0:T(8,128)(2,1)} %get-tuple-element.8.term_ref), custom_call_target="tpu_custom_call" | custom-call | tf_op jit(solution)/shard_map/gradient/pallas_call | solution.py:290
  (3 shorter events, 0.0 us)
Async XLA Ops:
  9.6 33.3 %copy-start.2 = (bf16[64,256]{1,0:T(8,128)(2,1)}, bf16[64,256]{1,0:T(8,128)(2,1)S(1)}, u32[]{:S(2)}) copy-start(bf16[64,256]{1,0:T(8,128)(2,1)S(1)} %get-tuple-element.16.sel_ref) | copy-start | bytes 98308
  9.6 33.3 %copy-start.3 = (bf16[64,256]{1,0:T(8,128)(2,1)}, bf16[64,256]{1,0:T(8,128)(2,1)S(1)}, u32[]{:S(2)}) copy-start(bf16[64,256]{1,0:T(8,128)(2,1)S(1)} %get-tuple-element.17.onehot_ref) | copy-start | bytes 98308
  42.9 61.7 %all-to-all-start = ((bf16[32,12,24,128]{3,2,1,0:T(8,128)(2,1)}), bf16[32,12,24,128]{3,2,1,0:T(8,128)(2,1)S(1)}, u32[]{:S(2)}, u32[]{:S(2)}) async-start(bf16[32,12,24,128]{3,2,1,0:T(8,128)(2,1)} %density.1), calls=%async_computation | async-start | bytes 4718592 | tf_op jit(solution)/shard_map/all_to_all | solution.py:251
  104.6 1.4 copy-start.1
  137.3 58.5 %all-to-all-start.1 = ((bf16[32,12,24,128]{3,2,1,0:T(8,128)(2,1)}), bf16[32,12,24,128]{3,2,1,0:T(8,128)(2,1)S(1)}, u32[]{:S(2)}, u32[]{:S(2)}) async-start(bf16[32,12,24,128]{3,2,1,0:T(8,128)(2,1)} %bitcast.9), calls=%async_computation.1 | async-start | bytes 4718592 | tf_op jit(solution)/shard_map/all_to_all | solution.py:268
  141.4 256.0 %all-reduce.2.cloned.1.call-start = ((), (), s32[]{:S(2)}) async-start(), calls=%async_computation.2 | async-start | bytes 131072 | tf_op jit(solution)/shard_map/psum | solution.py:286
  195.8 1.4 copy-start
Sparse Core Ops, SparseCore 0:
  278.5 118.8 all-reduce.1

commit v2 on v1

--- a/solution.py
+++ b/solution.py
@@ -10,6 +10,7 @@
 
 B = 64
 LANES = 128
+GAP = 8
 BF = jnp.bfloat16
 F32 = jnp.float32
 VMEM_LIMIT = 56 * 1024 * 1024
@@ -32,14 +33,16 @@
     return hi, (a - hi.astype(F32)).astype(BF)
 
 
-def density_kernel(per_dev, ax_ref, onehot_ref, orb_ref, out_ref, scr):
+def density_kernel(per_dev, ax_ref, onehot_ref, orb_ref, out_ref, psi_ref, scr):
     _, rows, across, _ = orb_ref.shape
     pairs = onehot_ref.shape[0] // 2
+    pitch = pairs + GAP
     owners = pairs // per_dev
 
     def row(y, _):
         both = dot_nt(onehot_ref[...], orb_ref[0, y])
-        scr[pl.ds(pl.multiple_of(y * pairs, 8), pairs), :across] = both[:pairs] * both[pairs:]
+        scr[pl.ds(pl.multiple_of(y * pitch, 8), pairs), :across] = both[:pairs] * both[pairs:]
+        psi_ref[0, y] = both[pairs:].astype(BF)
         return 0
 
     lax.fori_loop(0, rows, row, 0, unroll=4)
@@ -51,7 +54,7 @@
             p = d * per_dev + s
             a = ax_ref[p]
             base = s * B
-            x = scr[pl.ds(p, rows, stride=pairs), :]
+            x = scr[pl.ds(p, rows, stride=pitch), :]
             near = pltpu.roll(x, lax.rem(base - a + 2 * LANES, LANES), 1)
             far = pltpu.roll(x, lax.rem(base + across - a + 2 * LANES, LANES), 1)
             rel = lane - base
@@ -67,6 +70,7 @@
     lane = lax.broadcasted_iota(jnp.int32, (B, LANES), 1)
     lane_all = lax.broadcasted_iota(jnp.int32, (extent, LANES), 1)
     slots = ring.shape[0]
+    pitch = B + GAP
 
     def along_rows(e):
         hi, lo = split(e)
@@ -91,7 +95,7 @@
             a = step * slots + slot
             d = cut(a, slot).astype(BF)
             e = dot_nn(jnp.concatenate([d, d], axis=1), sx2_ref[...])
-            field[pl.ds(pl.multiple_of(a * B, 8), B), :] = along_rows(e)
+            field[pl.ds(pl.multiple_of(a * pitch, 8), B), :] = along_rows(e)
         return 0
 
     lax.fori_loop(0, B // slots, first, 0)
@@ -99,9 +103,9 @@
     def middle(step, _):
         for k in range(4):
             y = step * 4 + k
-            e = along_rows(field[pl.ds(y, B, stride=B), :])
+            e = along_rows(field[pl.ds(y, B, stride=pitch), :])
             e = e / (lzx_ref[...] + ly_ref[y])
-            field[pl.ds(y, B, stride=B), :] = along_rows(e)
+            field[pl.ds(y, B, stride=pitch), :] = along_rows(e)
         return 0
 
     lax.fori_loop(0, B // 4, middle, 0)
@@ -109,7 +113,7 @@
     def last(step, _):
         for k in range(4):
             a = step * 4 + k
-            at = pl.ds(pl.multiple_of(a * B, 8), B)
+            at = pl.ds(pl.multiple_of(a * pitch, 8), B)
             hi, lo = split(along_rows(field[at, :]))
             field[at, :] = dot_nn(jnp.concatenate([hi, hi, lo], axis=1), sx3_ref[...])
         return 0
@@ -123,7 +127,7 @@
             out = jnp.zeros((extent, LANES), F32)
             for s in range(per_dev):
                 a = lax.rem(z - az_ref[s] + extent, extent)
-                v = field[pl.ds(pl.multiple_of(jnp.minimum(a, B - 1) * B, 8), B), :]
+                v = field[pl.ds(pl.multiple_of(jnp.minimum(a, B - 1) * pitch, 8), B), :]
                 v = jnp.where(a < B, v, 0.0)
                 ring[slot, s, :B] = v
                 ring[slot, s, extent:extent + B] = v
@@ -138,9 +142,10 @@
     lax.fori_loop(0, extent // slots, place, 0)
 
 
-def term_kernel(per_dev, ax_ref, live_ref, onehot_ref, same_ref, orb_ref, in_ref, term_ref, tile_ref, scr):
+def term_kernel(per_dev, ax_ref, live_ref, psi_ref, orb_ref, in_ref, term_ref, tile_ref, scr):
     _, rows, across, _ = orb_ref.shape
-    pairs = onehot_ref.shape[0]
+    pairs = psi_ref.shape[2]
+    pitch = pairs + GAP
     owners = pairs // per_dev
     lane = lax.broadcasted_iota(jnp.int32, (rows, LANES), 1)
 
@@ -156,7 +161,7 @@
             lit = live_ref[p] > 0
             v_p = jnp.where((rel >= 0) & (rel < B) & lit, near, 0.0)
             v_p = jnp.where((rel + across < B) & lit, far, v_p)
-            scr[pl.ds(p, rows, stride=pairs), :] = v_p
+            scr[pl.ds(p, rows, stride=pitch), :] = v_p
         return 0
 
     lax.fori_loop(0, owners, owner, 0, unroll=4)
@@ -170,25 +175,28 @@
     def row(i, acc):
         for k in range(step):
             y = i * step + k
-            o = orb_ref[0, y]
-            psi = dot_nt(onehot_ref[...], o)
-            t = (scr[pl.ds(pl.multiple_of(y * pairs, 8), pairs), :across] * psi).astype(BF)
+            v = scr[pl.ds(pl.multiple_of(y * pitch, 8), pairs), :across]
+            t = (v * psi_ref[0, y].astype(F32)).astype(BF)
             term_ref[0, y] = t
-            low = dot_nn(same_ref[...], t).astype(BF)
-            acc = acc + dot_nn(low, o)
+            acc = acc + dot_nn(t, orb_ref[0, y])
         return acc
 
     tile_ref[...] += lax.fori_loop(0, rows // step, row, jnp.zeros(tile_ref.shape, F32))
 
 
 def gradient_kernel(sel_ref, tiles_ref, orb_ref, term_ref, out_ref):
-    _, rows, _, _ = orb_ref.shape
-
-    def row(y, _):
-        out_ref[0, y] = dot_tn(term_ref[0, y], sel_ref[...]) - dot_nn(orb_ref[0, y], tiles_ref[...])
-        return 0
-
-    lax.fori_loop(0, rows, row, 0, unroll=4)
+    _, rows, across, norb = orb_ref.shape
+    step = 4 if rows % 4 == 0 else 1
+
+    def some(i, _):
+        at = pl.ds(i * step, step)
+        o = orb_ref[0, at].reshape(step * across, norb)
+        c = jnp.concatenate([term_ref[0, i * step + k].T for k in range(step)], axis=0)
+        total = dot_nn(c, sel_ref[...]) - dot_nn(o, tiles_ref[...])
+        out_ref[0, at] = total.reshape(step, across, norb)
+        return 0
+
+    lax.fori_loop(0, rows // step, some, 0, unroll=2)
 
 
 def tables(per_dev):
@@ -225,26 +233,22 @@
     hot_first = sel.astype(BF)
     hot_second = (seconds[:, None] == orbs[None, :]).astype(BF)
     hot_both = jnp.concatenate([hot_first, hot_second], axis=0)
-    equal = firsts[:, None] == firsts[None, :]
-    same = equal.astype(BF)
-    slot = jnp.arange(pairs)
-    leads = jnp.logical_not(jnp.any(equal & (slot[None, :] < slot[:, None]), axis=1))
-    lead_sel = (sel & leads[:, None]).astype(BF)
 
     smem = pl.BlockSpec(memory_space=pltpu.SMEM)
     full = lambda shape: pl.BlockSpec(shape, lambda z: (0,) * len(shape))
     orb_spec = pl.BlockSpec((1, rows, across, norb), lambda z: (z, 0, 0, 0))
     slab_spec = pl.BlockSpec((owners, 1, rows, LANES), lambda z: (0, z, 0, 0))
+    plane_spec = pl.BlockSpec((1, rows, pairs, across), lambda z: (z, 0, 0, 0))
     slab = jax.ShapeDtypeStruct((owners, depth, rows, LANES), BF)
     params = pltpu.CompilerParams(dimension_semantics=("arbitrary",), vmem_limit_bytes=VMEM_LIMIT)
 
-    density = pl.pallas_call(
+    density, psi = pl.pallas_call(
         functools.partial(density_kernel, per_dev),
         grid=(depth,),
-        out_shape=slab,
+        out_shape=(slab, jax.ShapeDtypeStruct((depth, rows, pairs, across), BF)),
         in_specs=[smem, full((2 * pairs, norb)), orb_spec],
-        out_specs=slab_spec,
-        scratch_shapes=[pltpu.VMEM((rows * pairs, LANES), F32)],
+        out_specs=(slab_spec, plane_spec),
+        scratch_shapes=[pltpu.VMEM((rows * (pairs + GAP), LANES), F32)],
         compiler_params=params,
         name="density",
     )(ax, hot_both, orbitals)
@@ -259,7 +263,7 @@
         in_specs=[smem, smem, smem, vmem, vmem, vmem, vmem, vmem],
         out_specs=vmem,
         scratch_shapes=[
-            pltpu.VMEM((B * B, LANES), F32),
+            pltpu.VMEM((B * (B + GAP), LANES), F32),
             pltpu.VMEM((4, per_dev, 2 * extent, LANES), F32),
         ],
         compiler_params=pltpu.CompilerParams(vmem_limit_bytes=VMEM_LIMIT),
@@ -274,18 +278,18 @@
             jax.ShapeDtypeStruct((depth, rows, pairs, across), BF),
             jax.ShapeDtypeStruct((pairs, norb), F32),
         ),
-        in_specs=[smem, smem, full((pairs, norb)), full((pairs, pairs)), orb_spec, slab_spec],
-        out_specs=(
-            pl.BlockSpec((1, rows, pairs, across), lambda z: (z, 0, 0, 0)),
-            full((pairs, norb)),
-        ),
-        scratch_shapes=[pltpu.VMEM((rows * pairs, LANES), F32)],
+        in_specs=[smem, smem, plane_spec, orb_spec, slab_spec],
+        out_specs=(plane_spec, full((pairs, norb))),
+        scratch_shapes=[pltpu.VMEM((rows * (pairs + GAP), LANES), F32)],
         compiler_params=params,
         name="term",
-    )(ax, pair_live, hot_second, same, orbitals, back)
-    summed = lax.psum(part, ("gz", "gy"))
-    rows_of = (summed / (float(B) ** 3 / 4.0)).astype(BF)
-    tiles = dot_tn(rows_of, lead_sel).astype(BF)
+    )(ax, pair_live, psi, orbitals, back)
+    shares = lax.all_to_all(part.reshape(owners, per_dev, norb), ("gz", "gy"), split_axis=0, concat_axis=0, tiled=True)
+    summed = lax.all_gather(jnp.sum(shares, axis=0), ("gz", "gy"), axis=0, tiled=True)
+    inner = lax.dot_general(
+        summed, sel.astype(F32), (((0,), (0,)), ((), ())), precision=lax.Precision.HIGHEST, preferred_element_type=F32
+    )
+    tiles = (inner / (float(B) ** 3 / 4.0)).astype(BF)
 
     return pl.pallas_call(
         gradient_kernel,
@@ -295,7 +299,7 @@
             full((pairs, norb)),
             full((norb, norb)),
             orb_spec,
-            pl.BlockSpec((1, rows, pairs, across), lambda z: (z, 0, 0, 0)),
+            plane_spec,
         ],
         out_specs=orb_spec,
         compiler_params=params,

time: 436 us -> 285 us (0.65)
  waiting for transfers between devices: 226 us -> 53.6 us
  blocking collectives: 0 us -> 107 us
  Pallas kernels: 172 us -> 109 us
  between operations: 13.5 us -> 0.06 us
    psum x1 -> x0, waiting for transfers between devices: 119 us -> none  [body(): summed = lax.psum(part, ('gz', 'gy'))]
    all_to_all x0 -> x2, blocking collectives: none -> 69.3 us  [the longest x1 59.8 us: body(): lax.all_to_all(potential.reshape(owners, depth, rows, LANES), ('gz', 'gy'...]
    pallas_call x1, Pallas kernels: 81.2 us -> 25.8 us  [body(): pl.pallas_call(functools.partial(term_kernel, per_dev), grid=(depth,), ou...]
    all_to_all x1 -> x0, waiting for transfers between devices: 53.6 us -> none  [body(): lax.all_to_all(potential.reshape(owners, depth, rows, LANES), ('gz', 'gy'...]
    all_gather x0 -> x1, blocking collectives: none -> 37.4 us  [body(): lax.all_gather(jnp.sum(shares, axis=0), ('gz', 'gy'), axis=0, tiled=True)]
  transfers between devices with their start and end apart: 3 -> 1, of which waited for: 3 -> 1; matrix products, arithmetic and copies ran while one was open for 0% -> 0% of each run, Pallas kernels for 0% -> 0%
where the time goes in v2:
time: 285 us; the launch traced here: 284 us
  Pallas kernels  109 us (38%)
  blocking collectives  107 us (38%)
  waiting for transfers between devices  53.6 us (19%)
  starting transfers between devices  7.33 us (3%)
  local copies, waits for them, and re-layouts  5.23 us (2%)
    all_to_all x1, blocking collectives, body(): lax.all_to_all(potential.reshape(owners, depth, rows, LANES), ('gz', 'gy'...  59.8 us
    all_to_all x1, waiting for transfers between devices, body(): lax.all_to_all(density, ('gz', 'gy'), split_axis=0, concat_axis=0, tiled=...  53.6 us
    all_gather x1, blocking collectives, body(): lax.all_gather(jnp.sum(shares, axis=0), ('gz', 'gy'), axis=0, tiled=True)  37.4 us
    pallas_call x1, Pallas kernels, body(): pl.pallas_call(functools.partial(poisson_kernel, per_dev, extent), out_sh...  30.1 us
    pallas_call x1, Pallas kernels, body(): pl.pallas_call(functools.partial(density_kernel, per_dev), grid=(depth,),...  29.3 us
    pallas_call x1, Pallas kernels, body(): pl.pallas_call(functools.partial(term_kernel, per_dev), grid=(depth,), ou...  25.8 us
    pallas_call x1, Pallas kernels, body(): pl.pallas_call(gradient_kernel, grid=(depth,), out_shape=jax.ShapeDtypeSt...  23.5 us
    all_to_all x1, blocking collectives, body(): lax.all_to_all(part.reshape(owners, per_dev, norb), ('gz', 'gy'), split_a...  9.49 us
  transfers between devices with their start and end apart: 1, of which 1 were waited for; matrix products, arithmetic and copies ran while one was open for 0% of the time, Pallas kernels for 0%

profile of v2, /device:TPU:0, one launch (start us, length us, event | category | flops | bytes accessed | tf_op | source)
XLA Modules:
  0.0 284.2 jit_solution(8681586673043521865)
XLA Ops:
  0.0 0.8 slice_bitcast_fusion
  0.8 0.8 copy.12
  1.6 0.6 gather_fusion
  2.2 0.7 slice_reduce_fusion.ax_ref
  2.9 0.1 fusion.1
  3.0 0.0 copy-start.1
  3.0 0.6 pad_maximum_fusion.onehot_ref
  3.6 29.3 %density.1 = (bf16[32,12,24,128]{3,2,1,0:T(8,128)(2,1)}, bf16[12,24,64,96]{3,2,1,0:T(8,128)(2,1)}) custom-call(s32[64]{0:T(128)} %slice_reduce_fusion.ax_ref, bf16[128,256]{1,0:T(8,128)(2,1)} %pad_maximum_fusion.onehot_ref, bf16[12,24,96,256]{3,2,1,0:T(8,128)(2,1)} %orb_ref.5), custom_call_target="tpu_custom_call" | custom-call | tf_op jit(solution)/shard_map/density/pallas_call | solution.py:245
  33.0 0.0 copy-done.1
  33.0 7.3 %all-to-all-start = ((bf16[32,12,24,128]{3,2,1,0:T(8,128)(2,1)}), bf16[32,12,24,128]{3,2,1,0:T(8,128)(2,1)S(1)}, u32[]{:S(2)}, u32[]{:S(2)}) async-start(bf16[32,12,24,128]{3,2,1,0:T(8,128)(2,1)} %get-tuple-element.10), calls=%async_computation | async-start | bytes 4718592 | tf_op jit(solution)/shard_map/all_to_all | solution.py:255
  40.3 0.8 slice_reduce_fusion.1
  41.1 53.6 %all-to-all-done = bf16[32,12,24,128]{3,2,1,0:T(8,128)(2,1)S(1)} async-done(((bf16[32,12,24,128]{3,2,1,0:T(8,128)(2,1)}), bf16[32,12,24,128]{3,2,1,0:T(8,128)(2,1)S(1)}, u32[]{:S(2)}, u32[]{:S(2)}) %all-to-all-start) | async-done | bytes 2359328 | tf_op jit(solution)/shard_map/all_to_all | solution.py:255
  94.7 0.0 copy-start
  94.7 1.4 copy-done
  96.1 30.1 %poisson.1 = bf16[8,4,12,24,128]{4,3,2,1,0:T(8,128)(2,1)} custom-call(s32[2]{0:T(128)} %get-tuple-element.14.az_ref, s32[2]{0:T(128)} %get-tuple-element.13.ay_ref, f32[64]{0:T(128)} %constant.35.clone.ly_ref, bf16[64,192]{1,0:T(8,128)(2,1)} %constant.36.clone.left_ref, bf16[256,128]{1,0:T(8,128)(2,1)} %constant.37.clone.sx2_ref, ...), custom_call_target="tpu_custom_call" | custom-call | tf_op jit(solution)/shard_map/poisson/pallas_call | solution.py:260
  126.2 59.8 %all_to_all.15.in_ref = bf16[32,12,24,128]{3,2,1,0:T(8,128)(2,1)} all-to-all(bf16[32,12,24,128]{3,2,1,0:T(8,128)(2,1)} %bitcast.11), channel_id=1, replica_groups=mesh['gz'=8,'gy'=4] {'gz','gy'}, dimensions={0} | all-to-all | bytes 4718592 | tf_op jit(solution)/shard_map/all_to_all | solution.py:272
  186.0 25.8 %term.1 = (bf16[12,24,64,96]{3,2,1,0:T(8,128)(2,1)}, f32[64,256]{1,0:T(8,128)}) custom-call(s32[64]{0:T(128)} %slice_reduce_fusion.ax_ref, s32[64]{0:T(128)} %live_ref.1, bf16[12,24,64,96]{3,2,1,0:T(8,128)(2,1)} %get-tuple-element.9.psi_ref, bf16[12,24,96,256]{3,2,1,0:T(8,128)(2,1)} %orb_ref.5, bf16[32,12,24,128]{3,2,1,0:T(8,128)(2,1)} %all_to_all.15.in_ref), custom_call_target="tpu_custom_call" | custom-call | tf_op jit(solution)/shard_map/term/pallas_call | solution.py:274
  211.8 0.9 reshape.11
  212.7 9.5 %all_to_all.16 = f32[32,2,256]{2,1,0:T(2,128)S(1)} all-to-all(f32[32,2,256]{2,1,0:T(2,128)S(1)} %reshape.11), channel_id=1, replica_groups=mesh['gz'=8,'gy'=4] {'gz','gy'}, dimensions={0} | all-to-all | bytes 131072 | tf_op jit(solution)/shard_map/all_to_all | solution.py:287
  222.2 37.4 %all-gather = f32[32,2,256]{2,1,0:T(2,128)S(1)} all-gather(f32[1,2,256]{2,1,0:T(2,128)S(1)} %bitcast.12), channel_id=1, replica_groups=mesh['gz'=8,'gy'=4] {'gz','gy'}, dimensions={0}, use_global_device_ids=true | all-gather | bytes 67584 | tf_op jit(solution)/shard_map/all_gather | solution.py:288
  259.7 1.0 fusion.tiles_ref
  260.7 23.5 %gradient.1 = f32[12,24,96,256]{3,2,1,0:T(8,128)} custom-call(bf16[64,256]{1,0:T(8,128)(2,1)} %copy-done.1, bf16[256,256]{1,0:T(8,128)(2,1)} %fusion.tiles_ref, bf16[12,24,96,256]{3,2,1,0:T(8,128)(2,1)} %orb_ref.5, bf16[12,24,64,96]{3,2,1,0:T(8,128)(2,1)} %get-tuple-element.12.term_ref), custom_call_target="tpu_custom_call" | custom-call | tf_op jit(solution)/shard_map/gradient/pallas_call | solution.py:294
  (4 shorter events, 0.1 us)
Async XLA Ops:
  3.0 30.0 %copy-start.1 = (bf16[64,256]{1,0:T(8,128)(2,1)}, bf16[64,256]{1,0:T(8,128)(2,1)S(1)}, u32[]{:S(2)}) copy-start(bf16[64,256]{1,0:T(8,128)(2,1)S(1)} %get-tuple-element.18.sel_ref) | copy-start | bytes 98308
  33.0 61.7 %all-to-all-start = ((bf16[32,12,24,128]{3,2,1,0:T(8,128)(2,1)}), bf16[32,12,24,128]{3,2,1,0:T(8,128)(2,1)S(1)}, u32[]{:S(2)}, u32[]{:S(2)}) async-start(bf16[32,12,24,128]{3,2,1,0:T(8,128)(2,1)} %get-tuple-element.10), calls=%async_computation | async-start | bytes 4718592 | tf_op jit(solution)/shard_map/all_to_all | solution.py:255
  94.7 1.4 copy-start

commit v3 on v2

--- a/solution.py
+++ b/solution.py
@@ -65,8 +65,19 @@
     lax.fori_loop(0, owners, owner, 0, unroll=4)
 
 
-def poisson_kernel(per_dev, extent, az_ref, ay_ref, ly_ref, left_ref, sx2_ref, sx3_ref, lzx_ref, in_ref, out_ref, field, ring):
+def poisson_kernel(per_dev, extent, chunks, az_ref, ay_ref, ly_ref, left_ref, sx2_ref, sx3_ref, lzx_ref, *refs):
+    parts = refs[:len(chunks)]
+    outs = refs[len(chunks):2 * len(chunks)]
+    in_ref, field, ring, sems = refs[2 * len(chunks):]
     n_gz, n_gy, depth, rows, _ = in_ref.shape
+    copies = [
+        pltpu.make_async_copy(part, in_ref.at[:, :, start:start + size], sems.at[k])
+        for k, (part, (start, size)) in enumerate(zip(parts, chunks))
+    ]
+    for copy in copies:
+        copy.start()
+    for copy in copies:
+        copy.wait()
     lane = lax.broadcasted_iota(jnp.int32, (B, LANES), 1)
     lane_all = lax.broadcasted_iota(jnp.int32, (extent, LANES), 1)
     slots = ring.shape[0]
@@ -121,29 +132,34 @@
     lax.fori_loop(0, B // 4, last, 0)
     ring[...] = jnp.zeros_like(ring)
 
-    def place(step, _):
-        for slot in range(slots):
-            z = step * slots + slot
-            out = jnp.zeros((extent, LANES), F32)
-            for s in range(per_dev):
-                a = lax.rem(z - az_ref[s] + extent, extent)
-                v = field[pl.ds(pl.multiple_of(jnp.minimum(a, B - 1) * pitch, 8), B), :]
-                v = jnp.where(a < B, v, 0.0)
-                ring[slot, s, :B] = v
-                ring[slot, s, extent:extent + B] = v
-                got = ring[slot, s, pl.ds(extent - ay_ref[s], extent), :]
-                out = jnp.where(lane_all >= s * B, got, out)
-            gz = z // depth
-            zi = z - gz * depth
-            for gy in range(n_gy):
-                out_ref[gz, gy, zi] = out[gy * rows:(gy + 1) * rows].astype(BF)
-        return 0
-
-    lax.fori_loop(0, extent // slots, place, 0)
-
-
-def term_kernel(per_dev, ax_ref, live_ref, psi_ref, orb_ref, in_ref, term_ref, tile_ref, scr):
+    for out_ref, (start, size) in zip(outs, chunks):
+        group = slots if (n_gz * size) % slots == 0 else 1
+
+        def place(step, _):
+            for slot in range(group):
+                t = step * group + slot
+                gz = t // size
+                zi = t - gz * size
+                z = gz * depth + start + zi
+                out = jnp.zeros((extent, LANES), F32)
+                for s in range(per_dev):
+                    a = lax.rem(z - az_ref[s] + extent, extent)
+                    v = field[pl.ds(pl.multiple_of(jnp.minimum(a, B - 1) * pitch, 8), B), :]
+                    v = jnp.where(a < B, v, 0.0)
+                    ring[slot, s, :B] = v
+                    ring[slot, s, extent:extent + B] = v
+                    got = ring[slot, s, pl.ds(extent - ay_ref[s], extent), :]
+                    out = jnp.where(lane_all >= s * B, got, out)
+                for gy in range(n_gy):
+                    out_ref[gz, gy, zi] = out[gy * rows:(gy + 1) * rows].astype(BF)
+            return 0
+
+        lax.fori_loop(0, n_gz * size // group, place, 0)
+
+
+def term_kernel(per_dev, ax_ref, live_ref, psi_ref, orb_ref, in_ref, *refs):
     _, rows, across, _ = orb_ref.shape
+    term_ref, tile_ref, scr = refs[-3:]
     pairs = psi_ref.shape[2]
     pitch = pairs + GAP
     owners = pairs // per_dev
@@ -234,58 +250,89 @@
     hot_second = (seconds[:, None] == orbs[None, :]).astype(BF)
     hot_both = jnp.concatenate([hot_first, hot_second], axis=0)
 
+    half = max(depth // 2, 1)
+    chunks = [(start, size) for start, size in ((0, half), (half, depth - half)) if size]
     smem = pl.BlockSpec(memory_space=pltpu.SMEM)
+    vmem = pl.BlockSpec(memory_space=pltpu.VMEM)
+    hbm = pl.BlockSpec(memory_space=pl.ANY)
     full = lambda shape: pl.BlockSpec(shape, lambda z: (0,) * len(shape))
-    orb_spec = pl.BlockSpec((1, rows, across, norb), lambda z: (z, 0, 0, 0))
+    planes = lambda start, *dims: pl.BlockSpec((1,) + dims, lambda z: (z + start,) + (0,) * len(dims))
     slab_spec = pl.BlockSpec((owners, 1, rows, LANES), lambda z: (0, z, 0, 0))
-    plane_spec = pl.BlockSpec((1, rows, pairs, across), lambda z: (z, 0, 0, 0))
-    slab = jax.ShapeDtypeStruct((owners, depth, rows, LANES), BF)
     params = pltpu.CompilerParams(dimension_semantics=("arbitrary",), vmem_limit_bytes=VMEM_LIMIT)
-
-    density, psi = pl.pallas_call(
-        functools.partial(density_kernel, per_dev),
-        grid=(depth,),
-        out_shape=(slab, jax.ShapeDtypeStruct((depth, rows, pairs, across), BF)),
-        in_specs=[smem, full((2 * pairs, norb)), orb_spec],
-        out_specs=(slab_spec, plane_spec),
-        scratch_shapes=[pltpu.VMEM((rows * (pairs + GAP), LANES), F32)],
-        compiler_params=params,
-        name="density",
-    )(ax, hot_both, orbitals)
-    incoming = lax.all_to_all(density, ("gz", "gy"), split_axis=0, concat_axis=0, tiled=True)
-    incoming = incoming.reshape(n_gz, n_gy, depth, rows, LANES)
+    cells = rows * across
+
+    incoming, psis = [], []
+    for start, size in chunks:
+        density, psi = pl.pallas_call(
+            functools.partial(density_kernel, per_dev),
+            grid=(size,),
+            out_shape=(
+                jax.ShapeDtypeStruct((owners, size, rows, LANES), BF),
+                jax.ShapeDtypeStruct((size, rows, pairs, across), BF),
+            ),
+            in_specs=[smem, full((2 * pairs, norb)), planes(start, rows, across, norb)],
+            out_specs=(slab_spec, planes(0, rows, pairs, across)),
+            scratch_shapes=[pltpu.VMEM((rows * (pairs + GAP), LANES), F32)],
+            compiler_params=params,
+            cost_estimate=pl.CostEstimate(
+                flops=4 * size * cells * norb * pairs, bytes_accessed=16 * size * cells * norb, transcendentals=0
+            ),
+            name="density",
+        )(ax, hot_both, orbitals)
+        got = lax.all_to_all(density, ("gz", "gy"), split_axis=0, concat_axis=0, tiled=True)
+        incoming.append(got.reshape(n_gz, n_gy, size, rows, LANES))
+        psis.append(psi)
 
     eigen, left, sx2, sx3, lzx = tables(per_dev)
-    vmem = pl.BlockSpec(memory_space=pltpu.VMEM)
     potential = pl.pallas_call(
-        functools.partial(poisson_kernel, per_dev, extent),
-        out_shape=jax.ShapeDtypeStruct(incoming.shape, BF),
-        in_specs=[smem, smem, smem, vmem, vmem, vmem, vmem, vmem],
-        out_specs=vmem,
+        functools.partial(poisson_kernel, per_dev, extent, chunks),
+        out_shape=[jax.ShapeDtypeStruct(got.shape, BF) for got in incoming],
+        in_specs=[smem, smem, smem, vmem, vmem, vmem, vmem] + [hbm] * len(chunks),
+        out_specs=[vmem] * len(chunks),
         scratch_shapes=[
+            pltpu.VMEM((n_gz, n_gy, depth, rows, LANES), BF),
             pltpu.VMEM((B * (B + GAP), LANES), F32),
             pltpu.VMEM((4, per_dev, 2 * extent, LANES), F32),
+            pltpu.SemaphoreType.DMA((len(chunks),)),
         ],
         compiler_params=pltpu.CompilerParams(vmem_limit_bytes=VMEM_LIMIT),
         name="poisson",
-    )(mine[:, 0], mine[:, 1], jnp.asarray(eigen), jnp.asarray(left), jnp.asarray(sx2), jnp.asarray(sx3), jnp.asarray(lzx), incoming)
-    back = lax.all_to_all(potential.reshape(owners, depth, rows, LANES), ("gz", "gy"), split_axis=0, concat_axis=0, tiled=True)
-
-    term, part = pl.pallas_call(
-        functools.partial(term_kernel, per_dev),
-        grid=(depth,),
-        out_shape=(
-            jax.ShapeDtypeStruct((depth, rows, pairs, across), BF),
-            jax.ShapeDtypeStruct((pairs, norb), F32),
-        ),
-        in_specs=[smem, smem, plane_spec, orb_spec, slab_spec],
-        out_specs=(plane_spec, full((pairs, norb))),
-        scratch_shapes=[pltpu.VMEM((rows * (pairs + GAP), LANES), F32)],
-        compiler_params=params,
-        name="term",
-    )(ax, pair_live, psi, orbitals, back)
-    shares = lax.all_to_all(part.reshape(owners, per_dev, norb), ("gz", "gy"), split_axis=0, concat_axis=0, tiled=True)
-    summed = lax.all_gather(jnp.sum(shares, axis=0), ("gz", "gy"), axis=0, tiled=True)
+    )(mine[:, 0], mine[:, 1], jnp.asarray(eigen), jnp.asarray(left), jnp.asarray(sx2), jnp.asarray(sx3), jnp.asarray(lzx), *incoming)
+
+    term, part = None, 0.0
+    for (start, size), psi, field in zip(chunks, psis, potential):
+        back = lax.all_to_all(
+            field.reshape(owners, size, rows, LANES), ("gz", "gy"), split_axis=0, concat_axis=0, tiled=True
+        )
+        held = [] if term is None else [term]
+        term, share = pl.pallas_call(
+            functools.partial(term_kernel, per_dev),
+            grid=(size,),
+            out_shape=(
+                jax.ShapeDtypeStruct((depth, rows, pairs, across), BF),
+                jax.ShapeDtypeStruct((pairs, norb), F32),
+            ),
+            in_specs=[
+                smem,
+                smem,
+                planes(0, rows, pairs, across),
+                planes(start, rows, across, norb),
+                slab_spec,
+            ] + [hbm] * len(held),
+            out_specs=(planes(start, rows, pairs, across), full((pairs, norb))),
+            scratch_shapes=[pltpu.VMEM((rows * (pairs + GAP), LANES), F32)],
+            input_output_aliases={5: 0} if held else {},
+            compiler_params=params,
+            cost_estimate=pl.CostEstimate(
+                flops=2 * size * cells * norb * pairs, bytes_accessed=16 * size * cells * norb, transcendentals=0
+            ),
+            name="term",
+        )(ax, pair_live, psi, orbitals, back, *held)
+        part = part + share
+    whole = lambda x: lax.all_to_all(x, ("gz", "gy"), split_axis=0, concat_axis=0, tiled=True)
+    shares = whole(part.reshape(owners, per_dev, norb))
+    mine_sum = jnp.sum(shares, axis=0, keepdims=True)
+    summed = whole(jnp.broadcast_to(mine_sum, shares.shape)).reshape(pairs, norb)
     inner = lax.dot_general(
         summed, sel.astype(F32), (((0,), (0,)), ((), ())), precision=lax.Precision.HIGHEST, preferred_element_type=F32
     )
@@ -298,10 +345,10 @@
         in_specs=[
             full((pairs, norb)),
             full((norb, norb)),
-            orb_spec,
-            plane_spec,
+            planes(0, rows, across, norb),
+            planes(0, rows, pairs, across),
         ],
-        out_specs=orb_spec,
+        out_specs=planes(0, rows, across, norb),
         compiler_params=params,
         name="gradient",
     )(hot_first, tiles, orbitals, term)

time: 285 us -> 249 us (0.87)
  blocking collectives: 107 us -> 54.1 us
  starting transfers between devices: 7.33 us -> 13.6 us
  Pallas kernels: 109 us -> 114 us
  waiting for transfers between devices: 53.6 us -> 56.5 us
    all_gather x1 -> x0, blocking collectives: 37.4 us -> none  [body(): lax.all_gather(jnp.sum(shares, axis=0), ('gz', 'gy'), axis=0, tiled=True)]
    all_to_all x2 -> x3, blocking collectives: 69.3 us -> 54.1 us  [the longest x1 34.3 us: body(): lax.all_to_all(field.reshape(owners, size, rows, LANES), ('gz', 'gy'), sp...]
    all_to_all x0 -> x1, waiting for transfers between devices: none -> 15 us  [body(): lax.all_to_all(field.reshape(owners, size, rows, LANES), ('gz', 'gy'), sp...]
    all_to_all x1 -> x2, waiting for transfers between devices: 53.6 us -> 41.5 us  [body(): lax.all_to_all(density, ('gz', 'gy'), split_axis=0, concat_axis=0, tiled=...]
    pallas_call x3 -> x5, Pallas kernels: 85.2 us -> 90.5 us  [the longest x2 31.5 us: body(): pl.pallas_call(functools.partial(density_kernel, per_dev), grid=(size,),...]
    all_to_all x1 -> x2, starting transfers between devices: 7.33 us -> 10.9 us  [body(): lax.all_to_all(density, ('gz', 'gy'), split_axis=0, concat_axis=0, tiled=...]
  transfers between devices with their start and end apart: 1 -> 3, of which waited for: 1 -> 3; matrix products, arithmetic and copies ran while one was open for 0% -> 0% of each run, Pallas kernels for 0% -> 12%
where the time goes in v3:
time: 249 us; the launch traced here: 248 us
  Pallas kernels  114 us (46%)
  waiting for transfers between devices  56.5 us (23%)
  blocking collectives  54.1 us (22%)
  starting transfers between devices  13.6 us (5%)
  local copies, waits for them, and re-layouts  6.13 us (2%)
    all_to_all x2, waiting for transfers between devices, body(): lax.all_to_all(density, ('gz', 'gy'), split_axis=0, concat_axis=0, tiled=...  41.5 us
    all_to_all x1, blocking collectives, body(): lax.all_to_all(field.reshape(owners, size, rows, LANES), ('gz', 'gy'), sp...  34.3 us
    pallas_call x2, Pallas kernels, body(): pl.pallas_call(functools.partial(density_kernel, per_dev), grid=(size,),...  31.5 us
    pallas_call x1, Pallas kernels, body(): pl.pallas_call(functools.partial(poisson_kernel, per_dev, extent, chunks)...  31 us
    pallas_call x2, Pallas kernels, body(): pl.pallas_call(functools.partial(term_kernel, per_dev), grid=(size,), out...  28 us
    pallas_call x1, Pallas kernels, body(): pl.pallas_call(gradient_kernel, grid=(depth,), out_shape=jax.ShapeDtypeSt...  23.5 us
    all_to_all x2, blocking collectives, body(): lax.all_to_all(x, ('gz', 'gy'), split_axis=0, concat_axis=0, tiled=True)  19.9 us
    all_to_all x1, waiting for transfers between devices, body(): lax.all_to_all(field.reshape(owners, size, rows, LANES), ('gz', 'gy'), sp...  15 us
  transfers between devices with their start and end apart: 3, of which 3 were waited for; matrix products, arithmetic and copies ran while one was open for 0% of the time, Pallas kernels for 12%

profile of v3, /device:TPU:0, one launch (start us, length us, event | category | flops | bytes accessed | tf_op | source)
XLA Modules:
  0.0 247.8 jit_solution(12266899417584777591)
XLA Ops:
  0.0 0.8 slice_bitcast_fusion
  0.8 0.8 copy.12
  1.6 0.6 gather_fusion
  2.2 0.7 slice_reduce_fusion.ax_ref
  2.9 0.1 fusion.1
  3.0 0.0 copy-start.3
  3.0 0.6 pad_maximum_fusion.onehot_ref
  3.7 15.7 %density.3 = (bf16[32,6,24,128]{3,2,1,0:T(8,128)(2,1)}, bf16[6,24,64,96]{3,2,1,0:T(8,128)(2,1)}) custom-call(s32[64]{0:T(128)} %slice_reduce_fusion.ax_ref, bf16[128,256]{1,0:T(8,128)(2,1)} %pad_maximum_fusion.onehot_ref, bf16[12,24,96,256]{3,2,1,0:T(8,128)(2,1)} %orb_ref.9), custom_call_target="tpu_custom_call" | custom-call | flops 905969664 | bytes 56623104 | tf_op jit(solution)/shard_map/density/pallas_call | solution.py:266
  19.4 0.0 copy-done.3
  19.4 7.3 %all-to-all-start.1 = ((bf16[32,6,24,128]{3,2,1,0:T(8,128)(2,1)}), bf16[32,6,24,128]{3,2,1,0:T(8,128)(2,1)S(1)}, u32[]{:S(2)}, u32[]{:S(2)}) async-start(bf16[32,6,24,128]{3,2,1,0:T(8,128)(2,1)} %get-tuple-element.17), calls=%async_computation.1 | async-start | bytes 2359296 | tf_op jit(solution)/shard_map/all_to_all | solution.py:282
  26.7 15.7 %density.2 = (bf16[32,6,24,128]{3,2,1,0:T(8,128)(2,1)}, bf16[6,24,64,96]{3,2,1,0:T(8,128)(2,1)}) custom-call(s32[64]{0:T(128)} %slice_reduce_fusion.ax_ref, bf16[128,256]{1,0:T(8,128)(2,1)} %pad_maximum_fusion.onehot_ref, bf16[12,24,96,256]{3,2,1,0:T(8,128)(2,1)} %orb_ref.9), custom_call_target="tpu_custom_call" | custom-call | flops 905969664 | bytes 56623104 | tf_op jit(solution)/shard_map/density/pallas_call | solution.py:266
  42.4 13.3 %all-to-all-done.1 = bf16[32,6,24,128]{3,2,1,0:T(8,128)(2,1)S(1)} async-done(((bf16[32,6,24,128]{3,2,1,0:T(8,128)(2,1)}), bf16[32,6,24,128]{3,2,1,0:T(8,128)(2,1)S(1)}, u32[]{:S(2)}, u32[]{:S(2)}) %all-to-all-start.1) | async-done | bytes 1179680 | tf_op jit(solution)/shard_map/all_to_all | solution.py:282
  55.7 0.0 copy-start.1
  55.8 1.0 copy-done.1
  56.8 3.6 %all-to-all-start = ((bf16[32,6,24,128]{3,2,1,0:T(8,128)(2,1)}), bf16[32,6,24,128]{3,2,1,0:T(8,128)(2,1)S(1)}, u32[]{:S(2)}, u32[]{:S(2)}) async-start(bf16[32,6,24,128]{3,2,1,0:T(8,128)(2,1)} %get-tuple-element.16), calls=%async_computation | async-start | bytes 2359296 | tf_op jit(solution)/shard_map/all_to_all | solution.py:282
  60.4 0.8 slice_reduce_fusion.1
  61.2 28.2 %all-to-all-done = bf16[32,6,24,128]{3,2,1,0:T(8,128)(2,1)S(1)} async-done(((bf16[32,6,24,128]{3,2,1,0:T(8,128)(2,1)}), bf16[32,6,24,128]{3,2,1,0:T(8,128)(2,1)S(1)}, u32[]{:S(2)}, u32[]{:S(2)}) %all-to-all-start) | async-done | bytes 1179680 | tf_op jit(solution)/shard_map/all_to_all | solution.py:282
  89.4 0.0 copy-start.2
  89.4 1.0 copy-done.2
  90.4 31.0 %poisson.1 = (bf16[8,4,6,24,128]{4,3,2,1,0:T(8,128)(2,1)}, bf16[8,4,6,24,128]{4,3,2,1,0:T(8,128)(2,1)}) custom-call(s32[2]{0:T(128)} %get-tuple-element.26.az_ref, s32[2]{0:T(128)} %get-tuple-element.25.ay_ref, f32[64]{0:T(128)} %constant.35.clone.ly_ref, bf16[64,192]{1,0:T(8,128)(2,1)} %constant.36.clone.left_ref, bf16[256,128]{1,0:T(8,128)(2,1)} %constant.37.clone.sx2_ref, ...), custom_call_target="tpu_custom_call" | custom-call | tf_op jit(solution)/shard_map/poisson/pallas_call | solution.py:287
  121.5 34.3 %all_to_all.30.in_ref = bf16[32,6,24,128]{3,2,1,0:T(8,128)(2,1)} all-to-all(bf16[32,6,24,128]{3,2,1,0:T(8,128)(2,1)} %bitcast.13), channel_id=1, replica_groups=mesh['gz'=8,'gy'=4] {'gz','gy'}, dimensions={0} | all-to-all | bytes 2359296 | tf_op jit(solution)/shard_map/all_to_all | solution.py:304
  155.7 2.7 %all-to-all-start.3 = ((bf16[32,6,24,128]{3,2,1,0:T(8,128)(2,1)}), bf16[32,6,24,128]{3,2,1,0:T(8,128)(2,1)S(1)}, u32[]{:S(2)}, u32[]{:S(2)}) async-start(bf16[32,6,24,128]{3,2,1,0:T(8,128)(2,1)} %bitcast.6), calls=%async_computation.3 | async-start | bytes 2359296 | tf_op jit(solution)/shard_map/all_to_all | solution.py:304
  158.4 14.0 %term.2 = (bf16[12,24,64,96]{3,2,1,0:T(8,128)(2,1)}, f32[64,256]{1,0:T(8,128)}) custom-call(s32[64]{0:T(128)} %slice_reduce_fusion.ax_ref, s32[64]{0:T(128)} %live_ref.3, bf16[6,24,64,96]{3,2,1,0:T(8,128)(2,1)} %get-tuple-element.15.psi_ref, bf16[12,24,96,256]{3,2,1,0:T(8,128)(2,1)} %orb_ref.9, bf16[32,6,24,128]{3,2,1,0:T(8,128)(2,1)} %all_to_all.30.in_ref), custom_call_target="tpu_custom_call" | custom-call | flops 452984832 | bytes 56623104 | tf_op jit(solution)/shard_map/term/pallas_call | solution.py:308
  172.4 15.0 %all-to-all-done.3.in_ref = bf16[32,6,24,128]{3,2,1,0:T(8,128)(2,1)S(1)} async-done(((bf16[32,6,24,128]{3,2,1,0:T(8,128)(2,1)}), bf16[32,6,24,128]{3,2,1,0:T(8,128)(2,1)S(1)}, u32[]{:S(2)}, u32[]{:S(2)}) %all-to-all-start.3) | async-done | bytes 1179680 | tf_op jit(solution)/shard_map/all_to_all | solution.py:304
  187.4 1.0 copy-done
  188.4 14.1 %term.3 = (bf16[12,24,64,96]{3,2,1,0:T(8,128)(2,1)}, f32[64,256]{1,0:T(8,128)}) custom-call(s32[64]{0:T(128)} %slice_reduce_fusion.ax_ref, s32[64]{0:T(128)} %live_ref.3, bf16[6,24,64,96]{3,2,1,0:T(8,128)(2,1)} %get-tuple-element.20.psi_ref, bf16[12,24,96,256]{3,2,1,0:T(8,128)(2,1)} %orb_ref.9, ...), custom_call_target="tpu_custom_call", output_to_operand_aliasing={{0}: (5, {})} | custom-call | flops 452984832 | bytes 56623104 | tf_op jit(solution)/shard_map/term/pallas_call | solution.py:308
  202.5 0.0 copy-done.4
  202.5 0.8 add.20
  203.4 10.8 %all_to_all.31 = f32[32,2,256]{2,1,0:T(2,128)S(1)} all-to-all(f32[32,2,256]{2,1,0:T(2,128)S(1)} %reshape.23), channel_id=1, replica_groups=mesh['gz'=8,'gy'=4] {'gz','gy'}, dimensions={0} | all-to-all | bytes 131072 | tf_op jit(solution)/shard_map/all_to_all | solution.py:332
  214.2 9.1 %all_to_all.32 = f32[32,2,256]{2,1,0:T(2,128)S(1)} all-to-all(f32[32,2,256]{2,1,0:T(2,128)S(1)} %broadcast_in_dim.2), channel_id=1, replica_groups=mesh['gz'=8,'gy'=4] {'gz','gy'}, dimensions={0} | all-to-all | bytes 131072 | tf_op jit(solution)/shard_map/all_to_all | solution.py:332
  223.4 1.0 fusion.tiles_ref
  224.3 23.5 %gradient.1 = f32[12,24,96,256]{3,2,1,0:T(8,128)} custom-call(bf16[64,256]{1,0:T(8,128)(2,1)} %copy-done.3, bf16[256,256]{1,0:T(8,128)(2,1)} %fusion.tiles_ref, bf16[12,24,96,256]{3,2,1,0:T(8,128)(2,1)} %orb_ref.9, bf16[12,24,64,96]{3,2,1,0:T(8,128)(2,1)} %get-tuple-element.24.term_ref), custom_call_target="tpu_custom_call" | custom-call | tf_op jit(solution)/shard_map/gradient/pallas_call | solution.py:341
  (8 shorter events, 0.2 us)
Async XLA Ops:
  3.0 16.4 %copy-start.3 = (bf16[64,256]{1,0:T(8,128)(2,1)}, bf16[64,256]{1,0:T(8,128)(2,1)S(1)}, u32[]{:S(2)}) copy-start(bf16[64,256]{1,0:T(8,128)(2,1)S(1)} %get-tuple-element.30.sel_ref) | copy-start | bytes 98308
  19.4 36.3 %all-to-all-start.1 = ((bf16[32,6,24,128]{3,2,1,0:T(8,128)(2,1)}), bf16[32,6,24,128]{3,2,1,0:T(8,128)(2,1)S(1)}, u32[]{:S(2)}, u32[]{:S(2)}) async-start(bf16[32,6,24,128]{3,2,1,0:T(8,128)(2,1)} %get-tuple-element.17), calls=%async_computation.1 | async-start | bytes 2359296 | tf_op jit(solution)/shard_map/all_to_all | solution.py:282
  55.7 1.0 copy-start.1
  56.8 32.6 %all-to-all-start = ((bf16[32,6,24,128]{3,2,1,0:T(8,128)(2,1)}), bf16[32,6,24,128]{3,2,1,0:T(8,128)(2,1)S(1)}, u32[]{:S(2)}, u32[]{:S(2)}) async-start(bf16[32,6,24,128]{3,2,1,0:T(8,128)(2,1)} %get-tuple-element.16), calls=%async_computation | async-start | bytes 2359296 | tf_op jit(solution)/shard_map/all_to_all | solution.py:282
  89.4 1.0 copy-start.2
  155.7 31.7 %all-to-all-start.3 = ((bf16[32,6,24,128]{3,2,1,0:T(8,128)(2,1)}), bf16[32,6,24,128]{3,2,1,0:T(8,128)(2,1)S(1)}, u32[]{:S(2)}, u32[]{:S(2)}) async-start(bf16[32,6,24,128]{3,2,1,0:T(8,128)(2,1)} %bitcast.6), calls=%async_computation.3 | async-start | bytes 2359296 | tf_op jit(solution)/shard_map/all_to_all | solution.py:304
  187.4 1.0 copy-start
  188.4 14.1 %copy-start.4 = (f32[64,256]{1,0:T(8,128)S(1)}, f32[64,256]{1,0:T(8,128)}, u32[]{:S(2)}) copy-start(f32[64,256]{1,0:T(8,128)} %get-tuple-element.19) | copy-start | bytes 196612

commit v4 on v3

--- a/solution.py
+++ b/solution.py
@@ -39,13 +39,15 @@
     pitch = pairs + GAP
     owners = pairs // per_dev
 
-    def row(y, _):
+    def row(y, carry):
         both = dot_nt(onehot_ref[...], orb_ref[0, y])
-        scr[pl.ds(pl.multiple_of(y * pitch, 8), pairs), :across] = both[:pairs] * both[pairs:]
+        value = both[:pairs] * both[pairs:] + carry
+        sent = value.astype(BF).astype(F32)
+        scr[pl.ds(pl.multiple_of(y * pitch, 8), pairs), :across] = sent
         psi_ref[0, y] = both[pairs:].astype(BF)
-        return 0
-
-    lax.fori_loop(0, rows, row, 0, unroll=4)
+        return value - sent
+
+    lax.fori_loop(0, rows, row, jnp.zeros((pairs, across), F32), unroll=4)
     lane = lax.broadcasted_iota(jnp.int32, (rows, LANES), 1)
 
     def owner(d, _):
@@ -135,13 +137,14 @@
     for out_ref, (start, size) in zip(outs, chunks):
         group = slots if (n_gz * size) % slots == 0 else 1
 
-        def place(step, _):
+        def place(step, carry):
             for slot in range(group):
                 t = step * group + slot
                 gz = t // size
                 zi = t - gz * size
                 z = gz * depth + start + zi
                 out = jnp.zeros((extent, LANES), F32)
+                inside = jnp.zeros((extent, LANES), F32)
                 for s in range(per_dev):
                     a = lax.rem(z - az_ref[s] + extent, extent)
                     v = field[pl.ds(pl.multiple_of(jnp.minimum(a, B - 1) * pitch, 8), B), :]
@@ -150,11 +153,15 @@
                     ring[slot, s, extent:extent + B] = v
                     got = ring[slot, s, pl.ds(extent - ay_ref[s], extent), :]
                     out = jnp.where(lane_all >= s * B, got, out)
+                    inside = jnp.where(lane_all >= s * B, (a < B).astype(F32), inside)
+                out = out + carry * inside
+                sent = out.astype(BF)
+                carry = (out - sent.astype(F32)) * inside
                 for gy in range(n_gy):
-                    out_ref[gz, gy, zi] = out[gy * rows:(gy + 1) * rows].astype(BF)
-            return 0
-
-        lax.fori_loop(0, n_gz * size // group, place, 0)
+                    out_ref[gz, gy, zi] = sent[gy * rows:(gy + 1) * rows]
+            return carry
+
+        lax.fori_loop(0, n_gz * size // group, place, jnp.zeros((extent, LANES), F32))
 
 
 def term_kernel(per_dev, ax_ref, live_ref, psi_ref, orb_ref, in_ref, *refs):
@@ -250,8 +257,8 @@
     hot_second = (seconds[:, None] == orbs[None, :]).astype(BF)
     hot_both = jnp.concatenate([hot_first, hot_second], axis=0)
 
-    half = max(depth // 2, 1)
-    chunks = [(start, size) for start, size in ((0, half), (half, depth - half)) if size]
+    lead = max(depth // 3, 1)
+    chunks = [(start, size) for start, size in ((0, lead), (lead, depth - lead)) if size]
     smem = pl.BlockSpec(memory_space=pltpu.SMEM)
     vmem = pl.BlockSpec(memory_space=pltpu.VMEM)
     hbm = pl.BlockSpec(memory_space=pl.ANY)
@@ -300,7 +307,7 @@
     )(mine[:, 0], mine[:, 1], jnp.asarray(eigen), jnp.asarray(left), jnp.asarray(sx2), jnp.asarray(sx3), jnp.asarray(lzx), *incoming)
 
     term, part = None, 0.0
-    for (start, size), psi, field in zip(chunks, psis, potential):
+    for (start, size), psi, field in reversed(list(zip(chunks, psis, potential))):
         back = lax.all_to_all(
             field.reshape(owners, size, rows, LANES), ("gz", "gy"), split_axis=0, concat_axis=0, tiled=True
         )

time: 249 us -> 242 us (0.972)
  waiting for transfers between devices: 56.5 us -> 39.5 us
  blocking collectives: 54.1 us -> 62 us
  starting transfers between devices: 13.6 us -> 16.1 us
    all_to_all x1, waiting for transfers between devices: 15 us -> 2.57 us  [body(): lax.all_to_all(field.reshape(owners, size, rows, LANES), ('gz', 'gy'), sp...]
    all_to_all x1, blocking collectives: 34.3 us -> 42.1 us  [body(): lax.all_to_all(field.reshape(owners, size, rows, LANES), ('gz', 'gy'), sp...]
    all_to_all x2, waiting for transfers between devices: 41.5 us -> 36.9 us  [body(): lax.all_to_all(density, ('gz', 'gy'), split_axis=0, concat_axis=0, tiled=...]
  transfers between devices with their start and end apart: 3 -> 3, of which waited for: 3 -> 2; matrix products, arithmetic and copies ran while one was open for 0% -> 0% of each run, Pallas kernels for 12% -> 16%
where the time goes in v4:
time: 242 us; the launch traced here: 241 us
  Pallas kernels  115 us (48%)
  blocking collectives  62 us (26%)
  waiting for transfers between devices  39.5 us (16%)
  starting transfers between devices  16.1 us (7%)
  local copies, waits for them, and re-layouts  5.07 us (2%)
    all_to_all x1, blocking collectives, body(): lax.all_to_all(field.reshape(owners, size, rows, LANES), ('gz', 'gy'), sp...  42.1 us
    all_to_all x2, waiting for transfers between devices, body(): lax.all_to_all(density, ('gz', 'gy'), split_axis=0, concat_axis=0, tiled=...  36.9 us
    pallas_call x2, Pallas kernels, body(): pl.pallas_call(functools.partial(density_kernel, per_dev), grid=(size,),...  31.9 us
    pallas_call x1, Pallas kernels, body(): pl.pallas_call(functools.partial(poisson_kernel, per_dev, extent, chunks)...  31.3 us
    pallas_call x2, Pallas kernels, body(): pl.pallas_call(functools.partial(term_kernel, per_dev), grid=(size,), out...  28.1 us
    pallas_call x1, Pallas kernels, body(): pl.pallas_call(gradient_kernel, grid=(depth,), out_shape=jax.ShapeDtypeSt...  23.5 us
    all_to_all x2, blocking collectives, body(): lax.all_to_all(x, ('gz', 'gy'), split_axis=0, concat_axis=0, tiled=True)  19.9 us
    all_to_all x2, starting transfers between devices, body(): lax.all_to_all(density, ('gz', 'gy'), split_axis=0, concat_axis=0, tiled=...  13.2 us
  transfers between devices with their start and end apart: 3, of which 2 were waited for; matrix products, arithmetic and copies ran while one was open for 0% of the time, Pallas kernels for 16%

profile of v4, /device:TPU:0, one launch (start us, length us, event | category | flops | bytes accessed | tf_op | source)
XLA Modules:
  0.0 240.9 jit_solution(2079169784501705014)
XLA Ops:
  0.0 0.8 slice_bitcast_fusion
  0.8 0.8 copy.12
  1.6 0.6 gather_fusion
  2.2 0.8 slice_reduce_fusion.ax_ref
  3.0 0.1 fusion.1
  3.1 0.0 copy-start.3
  3.1 0.6 pad_maximum_fusion.onehot_ref
  3.7 11.3 %density.3 = (bf16[32,4,24,128]{3,2,1,0:T(8,128)(2,1)}, bf16[4,24,64,96]{3,2,1,0:T(8,128)(2,1)}) custom-call(s32[64]{0:T(128)} %slice_reduce_fusion.ax_ref, bf16[128,256]{1,0:T(8,128)(2,1)} %pad_maximum_fusion.onehot_ref, bf16[12,24,96,256]{3,2,1,0:T(8,128)(2,1)} %orb_ref.9), custom_call_target="tpu_custom_call" | custom-call | flops 603979776 | bytes 37748736 | tf_op jit(solution)/shard_map/density/pallas_call | solution.py:273
  15.0 0.0 copy-done.3
  15.0 7.3 %all-to-all-start = ((bf16[32,4,24,128]{3,2,1,0:T(8,128)(2,1)}), bf16[32,4,24,128]{3,2,1,0:T(8,128)(2,1)S(1)}, u32[]{:S(2)}, u32[]{:S(2)}) async-start(bf16[32,4,24,128]{3,2,1,0:T(8,128)(2,1)} %get-tuple-element.16), calls=%async_computation | async-start | bytes 1572864 | tf_op jit(solution)/shard_map/all_to_all | solution.py:289
  22.3 20.6 %density.2 = (bf16[32,8,24,128]{3,2,1,0:T(8,128)(2,1)}, bf16[8,24,64,96]{3,2,1,0:T(8,128)(2,1)}) custom-call(s32[64]{0:T(128)} %slice_reduce_fusion.ax_ref, bf16[128,256]{1,0:T(8,128)(2,1)} %pad_maximum_fusion.onehot_ref, bf16[12,24,96,256]{3,2,1,0:T(8,128)(2,1)} %orb_ref.9), custom_call_target="tpu_custom_call" | custom-call | flops 1207959552 | bytes 75497472 | tf_op jit(solution)/shard_map/density/pallas_call | solution.py:273
  42.9 0.0 all-to-all-done
  42.9 0.0 copy-start.1
  42.9 5.8 %all-to-all-start.1 = ((bf16[32,8,24,128]{3,2,1,0:T(8,128)(2,1)}), bf16[32,8,24,128]{3,2,1,0:T(8,128)(2,1)S(1)}, u32[]{:S(2)}, u32[]{:S(2)}) async-start(bf16[32,8,24,128]{3,2,1,0:T(8,128)(2,1)} %get-tuple-element.17), calls=%async_computation.1 | async-start | bytes 3145728 | tf_op jit(solution)/shard_map/all_to_all | solution.py:289
  48.8 0.7 slice_reduce_fusion.1
  49.5 36.9 %all-to-all-done.1 = bf16[32,8,24,128]{3,2,1,0:T(8,128)(2,1)S(1)} async-done(((bf16[32,8,24,128]{3,2,1,0:T(8,128)(2,1)}), bf16[32,8,24,128]{3,2,1,0:T(8,128)(2,1)S(1)}, u32[]{:S(2)}, u32[]{:S(2)}) %all-to-all-start.1) | async-done | bytes 1572896 | tf_op jit(solution)/shard_map/all_to_all | solution.py:289
  86.4 0.0 copy-start
  86.4 0.0 copy-done.1
  86.4 1.2 copy-done
  87.6 31.3 %poisson.1 = (bf16[8,4,4,24,128]{4,3,2,1,0:T(8,128)(2,1)}, bf16[8,4,8,24,128]{4,3,2,1,0:T(8,128)(2,1)}) custom-call(s32[2]{0:T(128)} %get-tuple-element.26.az_ref, s32[2]{0:T(128)} %get-tuple-element.25.ay_ref, f32[64]{0:T(128)} %constant.35.clone.ly_ref, bf16[64,192]{1,0:T(8,128)(2,1)} %constant.36.clone.left_ref, bf16[256,128]{1,0:T(8,128)(2,1)} %constant.37.clone.sx2_ref, ...), custom_call_target="tpu_custom_call" | custom-call | tf_op jit(solution)/shard_map/poisson/pallas_call | solution.py:294
  118.9 42.1 %all_to_all.30.in_ref = bf16[32,8,24,128]{3,2,1,0:T(8,128)(2,1)} all-to-all(bf16[32,8,24,128]{3,2,1,0:T(8,128)(2,1)} %bitcast.13), channel_id=1, replica_groups=mesh['gz'=8,'gy'=4] {'gz','gy'}, dimensions={0} | all-to-all | bytes 3145728 | tf_op jit(solution)/shard_map/all_to_all | solution.py:311
  160.9 3.0 %all-to-all-start.3 = ((bf16[32,4,24,128]{3,2,1,0:T(8,128)(2,1)}), bf16[32,4,24,128]{3,2,1,0:T(8,128)(2,1)S(1)}, u32[]{:S(2)}, u32[]{:S(2)}) async-start(bf16[32,4,24,128]{3,2,1,0:T(8,128)(2,1)} %bitcast.6), calls=%async_computation.3 | async-start | bytes 1572864 | tf_op jit(solution)/shard_map/all_to_all | solution.py:311
  163.9 18.0 %term.2 = (bf16[12,24,64,96]{3,2,1,0:T(8,128)(2,1)}, f32[64,256]{1,0:T(8,128)}) custom-call(s32[64]{0:T(128)} %slice_reduce_fusion.ax_ref, s32[64]{0:T(128)} %live_ref.3, bf16[8,24,64,96]{3,2,1,0:T(8,128)(2,1)} %get-tuple-element.15.psi_ref, bf16[12,24,96,256]{3,2,1,0:T(8,128)(2,1)} %orb_ref.9, bf16[32,8,24,128]{3,2,1,0:T(8,128)(2,1)} %all_to_all.30.in_ref), custom_call_target="tpu_custom_call" | custom-call | flops 603979776 | bytes 75497472 | tf_op jit(solution)/shard_map/term/pallas_call | solution.py:315
  181.9 2.6 %all-to-all-done.3.in_ref = bf16[32,4,24,128]{3,2,1,0:T(8,128)(2,1)S(1)} async-done(((bf16[32,4,24,128]{3,2,1,0:T(8,128)(2,1)}), bf16[32,4,24,128]{3,2,1,0:T(8,128)(2,1)S(1)}, u32[]{:S(2)}, u32[]{:S(2)}) %all-to-all-start.3) | async-done | bytes 786464 | tf_op jit(solution)/shard_map/all_to_all | solution.py:311
  184.5 0.9 copy-done.2
  185.4 10.1 %term.3 = (bf16[12,24,64,96]{3,2,1,0:T(8,128)(2,1)}, f32[64,256]{1,0:T(8,128)}) custom-call(s32[64]{0:T(128)} %slice_reduce_fusion.ax_ref, s32[64]{0:T(128)} %live_ref.3, bf16[4,24,64,96]{3,2,1,0:T(8,128)(2,1)} %get-tuple-element.20.psi_ref, bf16[12,24,96,256]{3,2,1,0:T(8,128)(2,1)} %orb_ref.9, ...), custom_call_target="tpu_custom_call", output_to_operand_aliasing={{0}: (5, {})} | custom-call | flops 301989888 | bytes 37748736 | tf_op jit(solution)/shard_map/term/pallas_call | solution.py:315
  195.5 0.0 copy-done.4
  195.5 0.8 add.20
  196.4 10.8 %all_to_all.31 = f32[32,2,256]{2,1,0:T(2,128)S(1)} all-to-all(f32[32,2,256]{2,1,0:T(2,128)S(1)} %reshape.23), channel_id=1, replica_groups=mesh['gz'=8,'gy'=4] {'gz','gy'}, dimensions={0} | all-to-all | bytes 131072 | tf_op jit(solution)/shard_map/all_to_all | solution.py:339
  207.3 9.1 %all_to_all.32 = f32[32,2,256]{2,1,0:T(2,128)S(1)} all-to-all(f32[32,2,256]{2,1,0:T(2,128)S(1)} %broadcast_in_dim.2), channel_id=1, replica_groups=mesh['gz'=8,'gy'=4] {'gz','gy'}, dimensions={0} | all-to-all | bytes 131072 | tf_op jit(solution)/shard_map/all_to_all | solution.py:339
  216.4 1.0 fusion.tiles_ref
  217.4 23.5 %gradient.1 = f32[12,24,96,256]{3,2,1,0:T(8,128)} custom-call(bf16[64,256]{1,0:T(8,128)(2,1)} %copy-done.3, bf16[256,256]{1,0:T(8,128)(2,1)} %fusion.tiles_ref, bf16[12,24,96,256]{3,2,1,0:T(8,128)(2,1)} %orb_ref.9, bf16[12,24,64,96]{3,2,1,0:T(8,128)(2,1)} %get-tuple-element.24.term_ref), custom_call_target="tpu_custom_call" | custom-call | tf_op jit(solution)/shard_map/gradient/pallas_call | solution.py:348
  (8 shorter events, 0.2 us)
Async XLA Ops:
  3.1 11.9 %copy-start.3 = (bf16[64,256]{1,0:T(8,128)(2,1)}, bf16[64,256]{1,0:T(8,128)(2,1)S(1)}, u32[]{:S(2)}) copy-start(bf16[64,256]{1,0:T(8,128)(2,1)S(1)} %get-tuple-element.30.sel_ref) | copy-start | bytes 98308
  15.0 27.9 %all-to-all-start = ((bf16[32,4,24,128]{3,2,1,0:T(8,128)(2,1)}), bf16[32,4,24,128]{3,2,1,0:T(8,128)(2,1)S(1)}, u32[]{:S(2)}, u32[]{:S(2)}) async-start(bf16[32,4,24,128]{3,2,1,0:T(8,128)(2,1)} %get-tuple-element.16), calls=%async_computation | async-start | bytes 1572864 | tf_op jit(solution)/shard_map/all_to_all | solution.py:289
  42.9 43.5 %copy-start.1 = (bf16[32,4,24,128]{3,2,1,0:T(8,128)(2,1)}, bf16[32,4,24,128]{3,2,1,0:T(8,128)(2,1)S(1)}, u32[]{:S(2)}) copy-start(bf16[32,4,24,128]{3,2,1,0:T(8,128)(2,1)S(1)} %all-to-all-done) | copy-start | bytes 2359300
  42.9 43.5 %all-to-all-start.1 = ((bf16[32,8,24,128]{3,2,1,0:T(8,128)(2,1)}), bf16[32,8,24,128]{3,2,1,0:T(8,128)(2,1)S(1)}, u32[]{:S(2)}, u32[]{:S(2)}) async-start(bf16[32,8,24,128]{3,2,1,0:T(8,128)(2,1)} %get-tuple-element.17), calls=%async_computation.1 | async-start | bytes 3145728 | tf_op jit(solution)/shard_map/all_to_all | solution.py:289
  86.4 1.2 copy-start
  160.9 23.6 %all-to-all-start.3 = ((bf16[32,4,24,128]{3,2,1,0:T(8,128)(2,1)}), bf16[32,4,24,128]{3,2,1,0:T(8,128)(2,1)S(1)}, u32[]{:S(2)}, u32[]{:S(2)}) async-start(bf16[32,4,24,128]{3,2,1,0:T(8,128)(2,1)} %bitcast.6), calls=%async_computation.3 | async-start | bytes 1572864 | tf_op jit(solution)/shard_map/all_to_all | solution.py:311
  184.5 0.9 copy-start.2
  185.4 10.1 %copy-start.4 = (f32[64,256]{1,0:T(8,128)S(1)}, f32[64,256]{1,0:T(8,128)}, u32[]{:S(2)}) copy-start(f32[64,256]{1,0:T(8,128)} %get-tuple-element.19) | copy-start | bytes 196612

commit v5 on v4

--- a/solution.py
+++ b/solution.py
@@ -85,9 +85,10 @@
     slots = ring.shape[0]
     pitch = B + GAP
 
-    def along_rows(e):
-        hi, lo = split(e)
-        return dot_nn(left_ref[...], jnp.concatenate([hi, hi, lo], axis=0))
+    def along_rows(blocks):
+        hi, lo = split(jnp.concatenate(blocks, axis=1))
+        wide = dot_nn(left_ref[...], jnp.concatenate([hi, hi, lo], axis=0))
+        return [wide[:, k * LANES:(k + 1) * LANES] for k in range(len(blocks))]
 
     def cut(a, slot):
         out = None
@@ -104,34 +105,34 @@
         return out
 
     def first(step, _):
+        d = jnp.concatenate([cut(step * slots + slot, slot).astype(BF) for slot in range(slots)], axis=0)
+        e = dot_nn(jnp.concatenate([d, d], axis=1), sx2_ref[...])
+        moved = along_rows([e[slot * B:(slot + 1) * B] for slot in range(slots)])
         for slot in range(slots):
-            a = step * slots + slot
-            d = cut(a, slot).astype(BF)
-            e = dot_nn(jnp.concatenate([d, d], axis=1), sx2_ref[...])
-            field[pl.ds(pl.multiple_of(a * pitch, 8), B), :] = along_rows(e)
+            field[pl.ds(pl.multiple_of((step * slots + slot) * pitch, 8), B), :] = moved[slot]
         return 0
 
     lax.fori_loop(0, B // slots, first, 0)
 
     def middle(step, _):
-        for k in range(4):
-            y = step * 4 + k
-            e = along_rows(field[pl.ds(y, B, stride=pitch), :])
-            e = e / (lzx_ref[...] + ly_ref[y])
-            field[pl.ds(y, B, stride=pitch), :] = along_rows(e)
-        return 0
-
-    lax.fori_loop(0, B // 4, middle, 0)
+        at = [step * slots + k for k in range(slots)]
+        modes = along_rows([field[pl.ds(y, B, stride=pitch), :] for y in at])
+        solved = along_rows([e / (lzx_ref[...] + ly_ref[y]) for e, y in zip(modes, at)])
+        for y, e in zip(at, solved):
+            field[pl.ds(y, B, stride=pitch), :] = e
+        return 0
+
+    lax.fori_loop(0, B // slots, middle, 0, unroll=2)
 
     def last(step, _):
-        for k in range(4):
-            a = step * 4 + k
-            at = pl.ds(pl.multiple_of(a * pitch, 8), B)
-            hi, lo = split(along_rows(field[at, :]))
-            field[at, :] = dot_nn(jnp.concatenate([hi, hi, lo], axis=1), sx3_ref[...])
-        return 0
-
-    lax.fori_loop(0, B // 4, last, 0)
+        at = [pl.ds(pl.multiple_of((step * slots + k) * pitch, 8), B) for k in range(slots)]
+        hi, lo = split(jnp.concatenate(along_rows([field[a, :] for a in at]), axis=0))
+        e = dot_nn(jnp.concatenate([hi, hi, lo], axis=1), sx3_ref[...])
+        for k in range(slots):
+            field[at[k], :] = e[k * B:(k + 1) * B]
+        return 0
+
+    lax.fori_loop(0, B // slots, last, 0, unroll=2)
     ring[...] = jnp.zeros_like(ring)
 
     for out_ref, (start, size) in zip(outs, chunks):

time: 242 us -> 232 us (0.959)
  Pallas kernels: 115 us -> 105 us
    pallas_call x1, Pallas kernels: 31.3 us -> 21.7 us  [body(): pl.pallas_call(functools.partial(poisson_kernel, per_dev, extent, chunks)...]
  transfers between devices with their start and end apart: 3 -> 3, of which waited for: 2 -> 2; matrix products, arithmetic and copies ran while one was open for 0% -> 0% of each run, Pallas kernels for 16% -> 17%
where the time goes in v5:
time: 232 us; the launch traced here: 231 us
  Pallas kernels  105 us (45%)
  blocking collectives  61.9 us (27%)
  waiting for transfers between devices  39.5 us (17%)
  starting transfers between devices  16.1 us (7%)
  local copies, waits for them, and re-layouts  5.07 us (2%)
  other arithmetic  2.37 us (1%)
    all_to_all x1, blocking collectives, body(): lax.all_to_all(field.reshape(owners, size, rows, LANES), ('gz', 'gy'), sp...  42 us
    all_to_all x2, waiting for transfers between devices, body(): lax.all_to_all(density, ('gz', 'gy'), split_axis=0, concat_axis=0, tiled=...  36.9 us
    pallas_call x2, Pallas kernels, body(): pl.pallas_call(functools.partial(density_kernel, per_dev), grid=(size,),...  31.9 us
    pallas_call x2, Pallas kernels, body(): pl.pallas_call(functools.partial(term_kernel, per_dev), grid=(size,), out...  28.1 us
    pallas_call x1, Pallas kernels, body(): pl.pallas_call(gradient_kernel, grid=(depth,), out_shape=jax.ShapeDtypeSt...  23.5 us
    pallas_call x1, Pallas kernels, body(): pl.pallas_call(functools.partial(poisson_kernel, per_dev, extent, chunks)...  21.7 us
    all_to_all x2, blocking collectives, body(): lax.all_to_all(x, ('gz', 'gy'), split_axis=0, concat_axis=0, tiled=True)  19.9 us
    all_to_all x2, starting transfers between devices, body(): lax.all_to_all(density, ('gz', 'gy'), split_axis=0, concat_axis=0, tiled=...  13.2 us
  transfers between devices with their start and end apart: 3, of which 2 were waited for; matrix products, arithmetic and copies ran while one was open for 0% of the time, Pallas kernels for 17%

profile of v5, /device:TPU:0, one launch (start us, length us, event | category | flops | bytes accessed | tf_op | source)
XLA Modules:
  0.0 231.2 jit_solution(11961785982362258774)
XLA Ops:
  0.0 0.8 slice_bitcast_fusion
  0.8 0.8 copy.12
  1.6 0.6 gather_fusion
  2.2 0.8 slice_reduce_fusion.ax_ref
  3.0 0.1 fusion.1
  3.1 0.0 copy-start.3
  3.1 0.6 pad_maximum_fusion.onehot_ref
  3.7 11.3 %density.3 = (bf16[32,4,24,128]{3,2,1,0:T(8,128)(2,1)}, bf16[4,24,64,96]{3,2,1,0:T(8,128)(2,1)}) custom-call(s32[64]{0:T(128)} %slice_reduce_fusion.ax_ref, bf16[128,256]{1,0:T(8,128)(2,1)} %pad_maximum_fusion.onehot_ref, bf16[12,24,96,256]{3,2,1,0:T(8,128)(2,1)} %orb_ref.9), custom_call_target="tpu_custom_call" | custom-call | flops 603979776 | bytes 37748736 | tf_op jit(solution)/shard_map/density/pallas_call | solution.py:274
  15.0 0.0 copy-done.3
  15.0 7.3 %all-to-all-start = ((bf16[32,4,24,128]{3,2,1,0:T(8,128)(2,1)}), bf16[32,4,24,128]{3,2,1,0:T(8,128)(2,1)S(1)}, u32[]{:S(2)}, u32[]{:S(2)}) async-start(bf16[32,4,24,128]{3,2,1,0:T(8,128)(2,1)} %get-tuple-element.16), calls=%async_computation | async-start | bytes 1572864 | tf_op jit(solution)/shard_map/all_to_all | solution.py:290
  22.3 20.6 %density.2 = (bf16[32,8,24,128]{3,2,1,0:T(8,128)(2,1)}, bf16[8,24,64,96]{3,2,1,0:T(8,128)(2,1)}) custom-call(s32[64]{0:T(128)} %slice_reduce_fusion.ax_ref, bf16[128,256]{1,0:T(8,128)(2,1)} %pad_maximum_fusion.onehot_ref, bf16[12,24,96,256]{3,2,1,0:T(8,128)(2,1)} %orb_ref.9), custom_call_target="tpu_custom_call" | custom-call | flops 1207959552 | bytes 75497472 | tf_op jit(solution)/shard_map/density/pallas_call | solution.py:274
  42.9 0.0 all-to-all-done
  42.9 0.0 copy-start.1
  42.9 5.8 %all-to-all-start.1 = ((bf16[32,8,24,128]{3,2,1,0:T(8,128)(2,1)}), bf16[32,8,24,128]{3,2,1,0:T(8,128)(2,1)S(1)}, u32[]{:S(2)}, u32[]{:S(2)}) async-start(bf16[32,8,24,128]{3,2,1,0:T(8,128)(2,1)} %get-tuple-element.17), calls=%async_computation.1 | async-start | bytes 3145728 | tf_op jit(solution)/shard_map/all_to_all | solution.py:290
  48.8 0.7 slice_reduce_fusion.1
  49.5 36.9 %all-to-all-done.1 = bf16[32,8,24,128]{3,2,1,0:T(8,128)(2,1)S(1)} async-done(((bf16[32,8,24,128]{3,2,1,0:T(8,128)(2,1)}), bf16[32,8,24,128]{3,2,1,0:T(8,128)(2,1)S(1)}, u32[]{:S(2)}, u32[]{:S(2)}) %all-to-all-start.1) | async-done | bytes 1572896 | tf_op jit(solution)/shard_map/all_to_all | solution.py:290
  86.4 0.0 copy-start
  86.4 0.0 copy-done.1
  86.4 1.2 copy-done
  87.6 21.7 %poisson.1 = (bf16[8,4,4,24,128]{4,3,2,1,0:T(8,128)(2,1)}, bf16[8,4,8,24,128]{4,3,2,1,0:T(8,128)(2,1)}) custom-call(s32[2]{0:T(128)} %get-tuple-element.26.az_ref, s32[2]{0:T(128)} %get-tuple-element.25.ay_ref, f32[64]{0:T(128)} %constant.35.clone.ly_ref, bf16[64,192]{1,0:T(8,128)(2,1)} %constant.36.clone.left_ref, bf16[256,128]{1,0:T(8,128)(2,1)} %constant.37.clone.sx2_ref, ...), custom_call_target="tpu_custom_call" | custom-call | tf_op jit(solution)/shard_map/poisson/pallas_call | solution.py:295
  109.3 42.0 %all_to_all.30.in_ref = bf16[32,8,24,128]{3,2,1,0:T(8,128)(2,1)} all-to-all(bf16[32,8,24,128]{3,2,1,0:T(8,128)(2,1)} %bitcast.13), channel_id=1, replica_groups=mesh['gz'=8,'gy'=4] {'gz','gy'}, dimensions={0} | all-to-all | bytes 3145728 | tf_op jit(solution)/shard_map/all_to_all | solution.py:312
  151.3 3.0 %all-to-all-start.3 = ((bf16[32,4,24,128]{3,2,1,0:T(8,128)(2,1)}), bf16[32,4,24,128]{3,2,1,0:T(8,128)(2,1)S(1)}, u32[]{:S(2)}, u32[]{:S(2)}) async-start(bf16[32,4,24,128]{3,2,1,0:T(8,128)(2,1)} %bitcast.6), calls=%async_computation.3 | async-start | bytes 1572864 | tf_op jit(solution)/shard_map/all_to_all | solution.py:312
  154.3 18.0 %term.2 = (bf16[12,24,64,96]{3,2,1,0:T(8,128)(2,1)}, f32[64,256]{1,0:T(8,128)}) custom-call(s32[64]{0:T(128)} %slice_reduce_fusion.ax_ref, s32[64]{0:T(128)} %live_ref.3, bf16[8,24,64,96]{3,2,1,0:T(8,128)(2,1)} %get-tuple-element.15.psi_ref, bf16[12,24,96,256]{3,2,1,0:T(8,128)(2,1)} %orb_ref.9, bf16[32,8,24,128]{3,2,1,0:T(8,128)(2,1)} %all_to_all.30.in_ref), custom_call_target="tpu_custom_call" | custom-call | flops 603979776 | bytes 75497472 | tf_op jit(solution)/shard_map/term/pallas_call | solution.py:316
  172.3 2.6 %all-to-all-done.3.in_ref = bf16[32,4,24,128]{3,2,1,0:T(8,128)(2,1)S(1)} async-done(((bf16[32,4,24,128]{3,2,1,0:T(8,128)(2,1)}), bf16[32,4,24,128]{3,2,1,0:T(8,128)(2,1)S(1)}, u32[]{:S(2)}, u32[]{:S(2)}) %all-to-all-start.3) | async-done | bytes 786464 | tf_op jit(solution)/shard_map/all_to_all | solution.py:312
  174.9 0.9 copy-done.2
  175.7 10.1 %term.3 = (bf16[12,24,64,96]{3,2,1,0:T(8,128)(2,1)}, f32[64,256]{1,0:T(8,128)}) custom-call(s32[64]{0:T(128)} %slice_reduce_fusion.ax_ref, s32[64]{0:T(128)} %live_ref.3, bf16[4,24,64,96]{3,2,1,0:T(8,128)(2,1)} %get-tuple-element.20.psi_ref, bf16[12,24,96,256]{3,2,1,0:T(8,128)(2,1)} %orb_ref.9, ...), custom_call_target="tpu_custom_call", output_to_operand_aliasing={{0}: (5, {})} | custom-call | flops 301989888 | bytes 37748736 | tf_op jit(solution)/shard_map/term/pallas_call | solution.py:316
  185.8 0.0 copy-done.4
  185.8 0.8 add.20
  186.7 10.8 %all_to_all.31 = f32[32,2,256]{2,1,0:T(2,128)S(1)} all-to-all(f32[32,2,256]{2,1,0:T(2,128)S(1)} %reshape.23), channel_id=1, replica_groups=mesh['gz'=8,'gy'=4] {'gz','gy'}, dimensions={0} | all-to-all | bytes 131072 | tf_op jit(solution)/shard_map/all_to_all | solution.py:340
  197.6 9.1 %all_to_all.32 = f32[32,2,256]{2,1,0:T(2,128)S(1)} all-to-all(f32[32,2,256]{2,1,0:T(2,128)S(1)} %broadcast_in_dim.2), channel_id=1, replica_groups=mesh['gz'=8,'gy'=4] {'gz','gy'}, dimensions={0} | all-to-all | bytes 131072 | tf_op jit(solution)/shard_map/all_to_all | solution.py:340
  206.8 1.0 fusion.tiles_ref
  207.8 23.5 %gradient.1 = f32[12,24,96,256]{3,2,1,0:T(8,128)} custom-call(bf16[64,256]{1,0:T(8,128)(2,1)} %copy-done.3, bf16[256,256]{1,0:T(8,128)(2,1)} %fusion.tiles_ref, bf16[12,24,96,256]{3,2,1,0:T(8,128)(2,1)} %orb_ref.9, bf16[12,24,64,96]{3,2,1,0:T(8,128)(2,1)} %get-tuple-element.24.term_ref), custom_call_target="tpu_custom_call" | custom-call | tf_op jit(solution)/shard_map/gradient/pallas_call | solution.py:349
  (8 shorter events, 0.2 us)
Async XLA Ops:
  3.1 11.9 %copy-start.3 = (bf16[64,256]{1,0:T(8,128)(2,1)}, bf16[64,256]{1,0:T(8,128)(2,1)S(1)}, u32[]{:S(2)}) copy-start(bf16[64,256]{1,0:T(8,128)(2,1)S(1)} %get-tuple-element.30.sel_ref) | copy-start | bytes 98308
  15.0 27.9 %all-to-all-start = ((bf16[32,4,24,128]{3,2,1,0:T(8,128)(2,1)}), bf16[32,4,24,128]{3,2,1,0:T(8,128)(2,1)S(1)}, u32[]{:S(2)}, u32[]{:S(2)}) async-start(bf16[32,4,24,128]{3,2,1,0:T(8,128)(2,1)} %get-tuple-element.16), calls=%async_computation | async-start | bytes 1572864 | tf_op jit(solution)/shard_map/all_to_all | solution.py:290
  42.9 43.5 %copy-start.1 = (bf16[32,4,24,128]{3,2,1,0:T(8,128)(2,1)}, bf16[32,4,24,128]{3,2,1,0:T(8,128)(2,1)S(1)}, u32[]{:S(2)}) copy-start(bf16[32,4,24,128]{3,2,1,0:T(8,128)(2,1)S(1)} %all-to-all-done) | copy-start | bytes 2359300
  42.9 43.5 %all-to-all-start.1 = ((bf16[32,8,24,128]{3,2,1,0:T(8,128)(2,1)}), bf16[32,8,24,128]{3,2,1,0:T(8,128)(2,1)S(1)}, u32[]{:S(2)}, u32[]{:S(2)}) async-start(bf16[32,8,24,128]{3,2,1,0:T(8,128)(2,1)} %get-tuple-element.17), calls=%async_computation.1 | async-start | bytes 3145728 | tf_op jit(solution)/shard_map/all_to_all | solution.py:290
  86.4 1.2 copy-start
  151.3 23.6 %all-to-all-start.3 = ((bf16[32,4,24,128]{3,2,1,0:T(8,128)(2,1)}), bf16[32,4,24,128]{3,2,1,0:T(8,128)(2,1)S(1)}, u32[]{:S(2)}, u32[]{:S(2)}) async-start(bf16[32,4,24,128]{3,2,1,0:T(8,128)(2,1)} %bitcast.6), calls=%async_computation.3 | async-start | bytes 1572864 | tf_op jit(solution)/shard_map/all_to_all | solution.py:312
  174.9 0.9 copy-start.2
  175.7 10.1 %copy-start.4 = (f32[64,256]{1,0:T(8,128)S(1)}, f32[64,256]{1,0:T(8,128)}, u32[]{:S(2)}) copy-start(f32[64,256]{1,0:T(8,128)} %get-tuple-element.19) | copy-start | bytes 196612
